TPU v7x, 512 devices: a whole 4x8x8 slice. The times are simulated.
512 devices in a mesh: row: 32 (over x, y), col: 16 (over z, core).
Axes of the slice: x: 4, y: 8, z: 8, core: 2. Of those that a mesh axis runs over, the one named last changes fastest.
Arguments:
- inverse_block: float32 [16384, 16384], P('row', 'col'), may hold values from -6 to 6
- tile_list: int32 [32], replicated, may hold values from 0 to 63, as said below
- panels: bfloat16 [3, 16384, 512], P(None, 'row'), may hold values from -0.0625 to 0.0625
- links: bfloat16 [2, 512, 512], P(None, 'col'), may hold values from -0.25 to 0.25
- diag_inverse: float32 [3, 512, 512], P(None, None, 'col'), may hold values from -6 to 6
Outputs:
- panel_inverse: float32 [3, 16384, 512], P(None, 'row', 'col')
- cross_inverse: float32 [2, 512, 512], P(None, None, 'col')
- diag_block: float32 [3, 512, 512], P(None, None, 'col')
Inputs may be any that keep to these rules, and one draw needn't show every extreme that they name: `tile_list`: 32 different tile numbers in ascending order; for each g from 0 to 16 - 1, the aligned group of tiles g * (64 // 16) to (g + 1) * (64 // 16) - 1 holds at least one of them.
All inputs are finite; a program needn't handle non-finite values.
Results may differ from a plain program's by a relative error of at most 0.0003.
Values may be sent and summed in bfloat16 or wider, within the bound.
A program may use at most 64 MiB of HBM per device.

v0:
```python
import jax
import jax.numpy as jnp
from jax import lax
from jax.sharding import Mesh
from jax.sharding import PartitionSpec as P

ORDER = 16384
TILE = 256
ROW = ("row_0", "row_1")


precise = lax.Precision.HIGHEST


def from_root(array, axes, root):
    array = jnp.where(lax.axis_index(axes) == root, array, jnp.zeros_like(array))
    for axis in axes:
        array = lax.psum(array, axis)
    return array


def laid_out(blocks, dim):
    blocks = jnp.moveaxis(blocks, 0, dim)
    shape = blocks.shape
    return blocks.reshape(*shape[:dim], shape[dim] * shape[dim + 1], *shape[dim + 2 :])


def copy_for_each(array, axis):
    copies = jnp.broadcast_to(array, (lax.axis_size(axis), *array.shape))
    return lax.all_to_all(copies, axis, split_axis=0, concat_axis=0, tiled=True)


def gathered_copies(array, axis, dim):
    return laid_out(copy_for_each(array, axis), dim)


def split_up(array, dim, peers):
    shape = array.shape
    blocks = array.reshape(*shape[:dim], peers, shape[dim] // peers, *shape[dim + 1 :])
    return jnp.moveaxis(blocks, dim, 0)


def sent_and_summed(array, axis, dim):
    blocks = split_up(array, dim, lax.axis_size(axis))
    arrived = lax.all_to_all(blocks, axis, split_axis=0, concat_axis=0, tiled=True)
    return arrived.sum(axis=0)


def of_everyone(array, axis):
    everything = copy_for_each(array, axis)
    return jnp.sum(everything, axis=0)


def rows_for(lines, peers):
    spare = -len(lines) % peers
    return jnp.pad(lines, [(0, spare)] + [(0, 0)] * (lines.ndim - 1))


def total_of(array, axes):
    own = sent_and_summed(rows_for(array, lax.axis_size(axes)), axes, 0)
    whole = gathered_copies(own, axes, 0)
    return whole[: len(array)].reshape(array.shape)


def together(arrays, axis):
    ravelled, at, gathered = (jnp.concatenate([a.reshape(-1) for a in arrays]), 0, [])
    subtotal = total_of(ravelled, axis)
    for a in arrays:
        gathered.append(subtotal[at : at + a.size].reshape(a.shape))
        at += a.size
    return tuple(gathered)


def product(left, right):
    return jnp.dot(left, right, precision=precise, preferred_element_type=jnp.float32)


def local(inverse_block, tile_list, panels, links, diag_inverse):
    rows_here = inverse_block.shape[0]
    width_here = diag_inverse.shape[2]
    ratio = lax.axis_size(ROW) // lax.axis_size("col")
    row_number = lax.axis_index(ROW)
    col_number = lax.axis_index("col")
    tile_count = ORDER // TILE
    listed = jnp.any(
        tile_list[:, None] == jnp.arange(tile_count, dtype=jnp.int32)[None, :], axis=0
    ).astype(jnp.float32)
    tiles_here = rows_here // TILE
    mine = lax.dynamic_slice_in_dim(listed, row_number * tiles_here, tiles_here)
    row_mask = jnp.broadcast_to(mine[:, None], (tiles_here, TILE)).reshape(-1)
    supernodes = panels.shape[0]
    panel_parts = []
    cross_parts = []
    diag_parts = []
    previous = None
    diag_prev = None
    for supernode in range(supernodes):
        masked_panel = panels[supernode] * row_mask[:, None].astype(jnp.bfloat16)
        pieces = []
        for source in range(ratio):
            pieces.append(from_root(masked_panel, ROW, col_number * ratio + source))
        column_factor = jnp.concatenate(pieces, axis=0).astype(jnp.float32)
        local_factor = masked_panel.astype(jnp.float32)
        partial_rows = product(inverse_block, column_factor)
        if supernode > 0:
            link_block = gathered_copies(links[supernode - 1], "col", 0).astype(jnp.float32)
            link_share = lax.dynamic_slice_in_dim(
                link_block, col_number * width_here, width_here, 1
            )
            diag_full = lax.all_gather(diag_prev, "col", axis=1, tiled=True)
            factor_share = lax.dynamic_slice_in_dim(
                local_factor, col_number * width_here, width_here, 1
            )
            cross_term = product(previous.T, factor_share)
            carried = product(diag_full, link_share)
        current = sent_and_summed(partial_rows, "col", 1)
        if supernode > 0:
            current = current + product(previous, link_share)
        current = -current * row_mask[:, None]
        if supernode + 1 < supernodes:
            current_full = lax.all_gather(current, "col", axis=1, tiled=True)
        own_term = product(local_factor.T, current)
        if supernode == 0:
            diag_now = diag_inverse[supernode] - of_everyone(own_term, ROW)
        else:
            cross_sum, rest_sum = together(
                (cross_term, own_term - product(link_block.T, cross_term)), ROW
            )
            cross_block = -(cross_sum + carried)
            diag_now = diag_inverse[supernode] - rest_sum + product(link_block.T, carried)
        if supernode > 0:
            cross_parts.append(cross_block)
        panel_parts.append(current)
        diag_parts.append(diag_now)
        if supernode + 1 < supernodes:
            previous = current_full
        diag_prev = diag_now
    return (jnp.stack(panel_parts), jnp.stack(cross_parts), jnp.stack(diag_parts))


def solution(mesh):
    split = Mesh(mesh.devices.reshape(4, 8, mesh.shape["col"]), ("row_0", "row_1", "col"))
    return jax.shard_map(
        local,
        mesh=split,
        in_specs=(
            P(ROW, "col"),
            P(),
            P(None, ROW, None),
            P(None, "col", None),
            P(None, None, "col"),
        ),
        out_specs=(P(None, ROW, "col"), P(None, None, "col"), P(None, None, "col")),
        check_vma=False,
    )
```

profile of v0, /device:TPU:1, one launch (start us, length us, event | category | flops | bytes accessed | tf_op | source)
XLA Modules:
  0.0 481.7 jit_solution(13430602291217242635)
XLA Ops:
  7.2 0.9 fusion.33
  8.3 3.0 broadcast_select_fusion.5
  11.3 0.8 copy-done.1
  12.1 1.1 broadcast_select_fusion
  13.2 91.9 %all-reduce.7.cloned.1.call-done = (bf16[512,512]{1,0:T(8,128)(2,1)}, bf16[512,512]{1,0:T(8,128)(2,1)}, bf16[512,512]{1,0:T(8,128)(2,1)}, bf16[512,512]{1,0:T(8,...) async-done(((bf16[512,512]{1,0:T(8,128)(2,1)}, bf16[512,512]{1,0:T(8,128)(2,1)}, bf16[512,512]{1,0:T(8,128)(2,1)}, bf16[512,512]{1,0:T(8,128)(2,1)}, ...) | async-done | bytes 3145744 | tf_op jit(solution)/shard_map/psum | solution.py:18
  105.2 0.6 slice_bitcast_fusion
  105.8 0.9 broadcast_in_dim.24
  106.6 8.2 %all-to-all-start.2 = ((bf16[16,32,512]{2,1,0:T(8,128)(2,1)}), bf16[16,32,512]{2,1,0:T(8,128)(2,1)S(1)}, u32[]{:S(2)}, u32[]{:S(2)}) async-start(bf16[16,32,512]{2,1,0:T(8,128)(2,1)} %broadcast_in_dim.24), calls=%async_computation.2 | async-start | bytes 1048576 | tf_op jit(solution)/shard_map/all_to_all | solution.py:30
  114.9 89.4 %all-reduce.5.cloned.1.call-done = (bf16[512,512]{1,0:T(8,128)(2,1)}, bf16[512,512]{1,0:T(8,128)(2,1)}, bf16[512,512]{1,0:T(8,128)(2,1)}, bf16[512,512]{1,0:T(8,...) async-done(((bf16[512,512]{1,0:T(8,128)(2,1)}, bf16[512,512]{1,0:T(8,128)(2,1)}, bf16[512,512]{1,0:T(8,128)(2,1)}, bf16[512,512]{1,0:T(8,128)(2,1)}, ...) | async-done | bytes 3145744 | tf_op jit(solution)/shard_map/psum | solution.py:18
  204.3 4.4 fusion.9
  208.7 8.6 %all-to-all-start = ((f32[16,512,32]{1,2,0:T(8,128)}), f32[16,512,32]{1,2,0:T(8,128)}, u32[]{:S(2)}, u32[]{:S(2)}) async-start(f32[16,512,32]{1,2,0:T(8,128)} %bitcast.114), calls=%async_computation | async-start | bytes 2097152 | tf_op jit(solution)/shard_map/all_to_all | solution.py:45
  217.4 4.4 fusion.13
  221.8 23.7 %all-to-all-done = f32[16,512,32]{1,2,0:T(8,128)} async-done(((f32[16,512,32]{1,2,0:T(8,128)}), f32[16,512,32]{1,2,0:T(8,128)}, u32[]{:S(2)}, u32[]{:S(2)}) %all-to-all-start) | async-done | bytes 1048608 | tf_op jit(solution)/shard_map/all_to_all | solution.py:45
  245.5 4.2 all-to-all-start.1
  249.7 1.3 reduce_sum.56
  251.0 1.5 fusion.21
  252.5 24.4 %all-to-all-done.1 = f32[16,512,32]{1,2,0:T(8,128)} async-done(((f32[16,512,32]{1,2,0:T(8,128)}), f32[16,512,32]{1,2,0:T(8,128)}, u32[]{:S(2)}, u32[]{:S(2)}) %all-to-all-start.1) | async-done | bytes 1048608 | tf_op jit(solution)/shard_map/all_to_all | solution.py:45
  276.9 1.6 broadcast_in_dim.27
  278.5 7.2 %all-to-all-start.7 = ((f32[32,512,32]{1,2,0:T(8,128)}), f32[32,512,32]{1,2,0:T(8,128)}, u32[]{:S(2)}, u32[]{:S(2)}) async-start(f32[32,512,32]{1,2,0:T(8,128)} %broadcast_in_dim.27), calls=%async_computation.7 | async-start | bytes 4194304 | tf_op jit(solution)/shard_map/all_to_all | solution.py:30
  285.8 0.7 all-gather.5.cloned.1.call-update
  286.5 1.3 reduce_sum.57
  287.8 41.0 %all-gather.5.cloned.1.call-done = f32[512,512]{0,1:T(8,128)} async-done(((f32[512,32]{0,1:T(8,128)}), f32[512,512]{0,1:T(8,128)}) %all-gather.5.cloned.1.call-update) | async-done | bytes 1048592 | tf_op jit(solution)/shard_map/all_gather | solution.py:121
  328.8 1.7 fusion.3
  330.6 4.6 all-to-all-done.7
  335.2 1.7 reduce_sum.60
  336.9 1.5 bitcast_subtract_fusion.3
  338.4 2.5 fusion.25
  341.0 1.0 copy.28
  342.3 1.2 fusion.4
  343.9 0.8 copy.30
  344.7 7.0 %all-to-all-start.5 = ((f32[32,1,1024]{2,1,0:T(1,128)}), f32[32,1,1024]{2,1,0:T(1,128)S(1)}, u32[]{:S(2)}, u32[]{:S(2)}) async-start(f32[32,1,1024]{2,1,0:T(1,128)} %copy.30), calls=%async_computation.5 | async-start | bytes 262144 | tf_op jit(solution)/shard_map/all_to_all | solution.py:45
  351.7 4.4 fusion.17
  356.1 4.5 all-to-all-done.5
  360.7 6.2 %all-to-all-start.3 = ((f32[16,512,32]{1,2,0:T(8,128)}), f32[16,512,32]{1,2,0:T(8,128)}, u32[]{:S(2)}, u32[]{:S(2)}) async-start(f32[16,512,32]{1,2,0:T(8,128)} %bitcast.112), calls=%async_computation.3 | async-start | bytes 2097152 | tf_op jit(solution)/shard_map/all_to_all | solution.py:45
  366.9 0.5 all-gather.7.cloned.1.call-update
  367.5 27.5 %all-to-all-done.3 = f32[16,512,32]{1,2,0:T(8,128)} async-done(((f32[16,512,32]{1,2,0:T(8,128)}), f32[16,512,32]{1,2,0:T(8,128)}, u32[]{:S(2)}, u32[]{:S(2)}) %all-to-all-start.3) | async-done | bytes 1048608 | tf_op jit(solution)/shard_map/all_to_all | solution.py:45
  395.1 14.2 %all_to_all.60 = f32[32,1,1024]{2,1,0:T(1,128)S(1)} all-to-all(f32[32,1,1024]{2,1,0:T(1,128)S(1)} %broadcast_in_dim.26), channel_id=1, replica_groups=mesh['row_0'=4,'row_1'=8,'col'=16] {'row_0','row_1'}, dimensions={0} | all-to-all | bytes 262144 | tf_op jit(solution)/shard_map/all_to_all | solution.py:30
  409.3 0.8 broadcast_in_dim.25
  410.1 4.5 all-to-all-start.4
  414.7 1.9 reduce_sum.58
  416.6 0.8 slice_reduce_fusion.3
  417.7 1.8 fusion.30
  419.5 1.9 fusion.6
  421.3 5.7 %all-gather.7.cloned.1.call-done = f32[512,512]{0,1:T(8,128)} async-done(((f32[512,32]{0,1:T(8,128)}), f32[512,512]{0,1:T(8,128)}) %all-gather.7.cloned.1.call-update) | async-done | bytes 1048592 | tf_op jit(solution)/shard_map/all_gather | solution.py:121
  427.0 1.9 fusion.23
  429.0 3.1 all-to-all-done.4
  432.2 1.7 fusion.1
  434.6 1.2 fusion.5
  435.9 0.8 concatenate.32
  436.8 0.9 maximum_bitcast_fusion.1
  437.7 0.8 copy.34
  438.5 7.6 %all-to-all-start.8 = ((f32[32,1,1024]{2,1,0:T(1,128)}), f32[32,1,1024]{2,1,0:T(1,128)S(1)}, u32[]{:S(2)}, u32[]{:S(2)}) async-start(f32[32,1,1024]{2,1,0:T(1,128)} %copy.34), calls=%async_computation.8 | async-start | bytes 262144 | tf_op jit(solution)/shard_map/all_to_all | solution.py:45
  446.1 0.8 bitcast_multiply_fusion.4
  447.0 1.0 reshape.132
  448.0 7.2 %all-to-all-done.8 = f32[32,1,1024]{2,1,0:T(1,128)S(1)} async-done(((f32[32,1,1024]{2,1,0:T(1,128)}), f32[32,1,1024]{2,1,0:T(1,128)S(1)}, u32[]{:S(2)}, u32[]{:S(2)}) %all-to-all-start.8) | async-done | bytes 131104 | tf_op jit(solution)/shard_map/all_to_all | solution.py:45
  455.4 0.7 broadcast_in_dim.28
  456.1 4.4 all-to-all-start.9
  460.5 0.7 pad_maximum_fusion
  461.2 0.8 bitcast_subtract_fusion.1
  462.1 7.6 %all-to-all-done.9 = f32[32,1,1024]{2,1,0:T(1,128)S(1)} async-done(((f32[32,1,1024]{2,1,0:T(1,128)}), f32[32,1,1024]{2,1,0:T(1,128)S(1)}, u32[]{:S(2)}, u32[]{:S(2)}) %all-to-all-start.9) | async-done | bytes 131104 | tf_op jit(solution)/shard_map/all_to_all | solution.py:30
  470.5 1.7 fusion.27
  472.3 1.2 fusion.8
  473.5 0.7 pad_maximum_fusion.2
  474.2 0.7 pad_maximum_fusion.1
  (70 shorter events, 3.7 us)
Async XLA Ops:
  7.2 197.1 %copy-start = (f32[512,1024]{1,0:T(8,128)S(1)}, f32[512,1024]{1,0:T(8,128)}, u32[]{:S(2)}) copy-start(f32[512,1024]{1,0:T(8,128)} %param.5) | copy-start | bytes 6291460
  7.2 97.9 %all-reduce.7.cloned.1.call-start = ((), (), s32[]{:S(2)}) async-start(), calls=%async_computation.15 | async-start | bytes 6291456 | tf_op jit(solution)/shard_map/psum | solution.py:18
  11.3 0.8 copy-start.1
  13.2 92.0 %copy-start.14 = (bf16[2,32,512]{2,1,0:T(8,128)(2,1)S(1)}, bf16[2,32,512]{2,1,0:T(8,128)(2,1)}, u32[]{:S(2)}) copy-start(bf16[2,32,512]{2,1,0:T(8,128)(2,1)} %param.8) | copy-start | bytes 196612
  13.2 191.1 %all-reduce.5.cloned.1.call-start = ((), (), s32[]{:S(2)}) async-start(), calls=%async_computation.14 | async-start | bytes 6291456 | tf_op jit(solution)/shard_map/psum | solution.py:18
  106.6 102.1 %all-to-all-start.2 = ((bf16[16,32,512]{2,1,0:T(8,128)(2,1)}), bf16[16,32,512]{2,1,0:T(8,128)(2,1)S(1)}, u32[]{:S(2)}, u32[]{:S(2)}) async-start(bf16[16,32,512]{2,1,0:T(8,128)(2,1)} %broadcast_in_dim.24), calls=%async_computation.2 | async-start | bytes 1048576 | tf_op jit(solution)/shard_map/all_to_all | solution.py:30
  208.7 36.7 %all-to-all-start = ((f32[16,512,32]{1,2,0:T(8,128)}), f32[16,512,32]{1,2,0:T(8,128)}, u32[]{:S(2)}, u32[]{:S(2)}) async-start(f32[16,512,32]{1,2,0:T(8,128)} %bitcast.114), calls=%async_computation | async-start | bytes 2097152 | tf_op jit(solution)/shard_map/all_to_all | solution.py:45
  245.5 31.5 %all-to-all-start.1 = ((f32[16,512,32]{1,2,0:T(8,128)}), f32[16,512,32]{1,2,0:T(8,128)}, u32[]{:S(2)}, u32[]{:S(2)}) async-start(f32[16,512,32]{1,2,0:T(8,128)} %bitcast.113), calls=%async_computation.1 | async-start | bytes 2097152 | tf_op jit(solution)/shard_map/all_to_all | solution.py:45
  251.0 27.5 %copy-start.7 = (f32[512,32]{0,1:T(8,128)}, f32[512,32]{0,1:T(8,128)S(1)}, u32[]{:S(2)}) copy-start(f32[512,32]{0,1:T(8,128)S(1)} %reduce_sum.56) | copy-start | bytes 196612
  251.0 27.5 %copy-start.12 = (f32[512,32]{0,1:T(8,128)}, f32[512,32]{0,1:T(8,128)S(1)}, u32[]{:S(2)}) copy-start(f32[512,32]{0,1:T(8,128)S(1)} %negate_multiply_fusion) | copy-start | bytes 196612
  278.5 56.7 %all-to-all-start.7 = ((f32[32,512,32]{1,2,0:T(8,128)}), f32[32,512,32]{1,2,0:T(8,128)}, u32[]{:S(2)}, u32[]{:S(2)}) async-start(f32[32,512,32]{1,2,0:T(8,128)} %broadcast_in_dim.27), calls=%async_computation.7 | async-start | bytes 4194304 | tf_op jit(solution)/shard_map/all_to_all | solution.py:30
  285.7 43.0 %all-gather.5.cloned.1.call-start = ((), (), s32[]{:S(2)}) async-start(), calls=%async_computation.10 | async-start | bytes 1114112 | tf_op jit(solution)/shard_map/all_gather | solution.py:121
  286.5 131.2 %all-gather.9.cloned.1.call-start = ((), (), s32[]{:S(2)}) async-start(), calls=%async_computation.12 | async-start | bytes 1114112 | tf_op jit(solution)/shard_map/all_gather | solution.py:110
  330.5 11.7 %copy-start.3 = (f32[512,32]{0,1:T(8,128)}, f32[512,32]{0,1:T(8,128)S(1)}, u32[]{:S(2)}) copy-start(f32[512,32]{0,1:T(8,128)S(1)} %fusion.3) | copy-start | bytes 196612
  344.7 15.9 %all-to-all-start.5 = ((f32[32,1,1024]{2,1,0:T(1,128)}), f32[32,1,1024]{2,1,0:T(1,128)S(1)}, u32[]{:S(2)}, u32[]{:S(2)}) async-start(f32[32,1,1024]{2,1,0:T(1,128)} %copy.30), calls=%async_computation.5 | async-start | bytes 262144 | tf_op jit(solution)/shard_map/all_to_all | solution.py:45
  356.1 53.2 %copy-start.13 = (bf16[32,512]{1,0:T(8,128)(2,1)S(1)}, bf16[32,512]{1,0:T(8,128)(2,1)}, u32[]{:S(2)}) copy-start(bf16[32,512]{1,0:T(8,128)(2,1)} %get-tuple-element.29) | copy-start | bytes 98308
  360.7 34.3 %all-to-all-start.3 = ((f32[16,512,32]{1,2,0:T(8,128)}), f32[16,512,32]{1,2,0:T(8,128)}, u32[]{:S(2)}, u32[]{:S(2)}) async-start(f32[16,512,32]{1,2,0:T(8,128)} %bitcast.112), calls=%async_computation.3 | async-start | bytes 2097152 | tf_op jit(solution)/shard_map/all_to_all | solution.py:45
  366.8 60.2 %all-gather.7.cloned.1.call-start = ((), (), s32[]{:S(2)}) async-start(), calls=%async_computation.11 | async-start | bytes 1114112 | tf_op jit(solution)/shard_map/all_gather | solution.py:121
  410.1 22.0 %all-to-all-start.4 = ((bf16[16,32,512]{2,1,0:T(8,128)(2,1)}), bf16[16,32,512]{2,1,0:T(8,128)(2,1)S(1)}, u32[]{:S(2)}, u32[]{:S(2)}) async-start(bf16[16,32,512]{2,1,0:T(8,128)(2,1)} %broadcast_in_dim.25), calls=%async_computation.4 | async-start | bytes 1048576 | tf_op jit(solution)/shard_map/all_to_all | solution.py:30
  414.6 55.9 %all-gather.11.cloned.1.call-start = ((), (), s32[]{:S(2)}) async-start(), calls=%async_computation.13 | async-start | bytes 1114112 | tf_op jit(solution)/shard_map/all_gather | solution.py:110
  419.4 7.5 %copy-start.5 = (f32[512,32]{0,1:T(8,128)}, f32[512,32]{0,1:T(8,128)S(1)}, u32[]{:S(2)}) copy-start(f32[512,32]{0,1:T(8,128)S(1)} %fusion.30) | copy-start | bytes 196612
  421.3 12.6 %copy-start.2 = (bf16[512,512]{1,0:T(8,128)(2,1)S(1)}, bf16[512,512]{1,0:T(8,128)(2,1)}, u32[]{:S(2)}) copy-start(bf16[512,512]{1,0:T(8,128)(2,1)} %copy-done.1) | copy-start | bytes 1572868
  428.9 3.3 copy-start.11
  433.9 0.6 copy-start.8
  433.9 26.6 %copy-start.4 = (f32[512,32]{0,1:T(8,128)S(1)}, f32[512,32]{0,1:T(8,128)}, u32[]{:S(2)}) copy-start(f32[512,32]{0,1:T(8,128)} %copy-done.3) | copy-start | bytes 196612
  435.8 24.8 %copy-start.9 = (f32[512,32]{0,1:T(8,128)S(1)}, f32[512,32]{0,1:T(8,128)}, u32[]{:S(2)}) copy-start(f32[512,32]{0,1:T(8,128)} %copy-done.8) | copy-start | bytes 196612
  436.8 33.6 %copy-start.6 = (f32[512,32]{0,1:T(8,128)S(1)}, f32[512,32]{0,1:T(8,128)}, u32[]{:S(2)}) copy-start(f32[512,32]{0,1:T(8,128)} %copy-done.5) | copy-start | bytes 196612
  438.5 16.8 %all-to-all-start.8 = ((f32[32,1,1024]{2,1,0:T(1,128)}), f32[32,1,1024]{2,1,0:T(1,128)S(1)}, u32[]{:S(2)}, u32[]{:S(2)}) async-start(f32[32,1,1024]{2,1,0:T(1,128)} %copy.34), calls=%async_computation.8 | async-start | bytes 262144 | tf_op jit(solution)/shard_map/all_to_all | solution.py:45
  456.1 13.6 %all-to-all-start.9 = ((f32[32,1,1024]{2,1,0:T(1,128)}), f32[32,1,1024]{2,1,0:T(1,128)S(1)}, u32[]{:S(2)}, u32[]{:S(2)}) async-start(f32[32,1,1024]{2,1,0:T(1,128)} %broadcast_in_dim.28), calls=%async_computation.9 | async-start | bytes 262144 | tf_op jit(solution)/shard_map/all_to_all | solution.py:30
  462.1 12.1 %copy-start.10 = (f32[512,32]{0,1:T(8,128)S(1)}, f32[512,32]{0,1:T(8,128)}, u32[]{:S(2)}) copy-start(f32[512,32]{0,1:T(8,128)} %fusion.6) | copy-start | bytes 196612
Sparse Core Ops, SparseCore 0:
  13.3 91.7 all-reduce.6
  107.9 96.3 all-reduce.4
  289.2 39.4 all-gather.4
  338.6 37.9 all-gather.8
  379.1 47.8 all-gather.6
  429.0 41.4 all-gather.10
where the time goes:
time: 484 us; the launch traced here: 482 us
  waiting for transfers between devices  332 us (69%)
  starting transfers between devices  58.2 us (12%)
  matrix products  32.3 us (7%)
  other arithmetic  17.6 us (4%)
  between operations  14.5 us (3%)
  blocking collectives  14.2 us (3%)
  local copies, waits for them, and re-layouts  12.9 us (3%)
    psum x2, waiting for transfers between devices, from_root(): array = lax.psum(array, axis)  181 us
    all_to_all x5, waiting for transfers between devices, sent_and_summed(): lax.all_to_all(blocks, axis, split_axis=0, concat_axis=0, tiled=True)  87.3 us
    all_gather x2, waiting for transfers between devices, local(): current_full = lax.all_gather(current, 'col', axis=1, tiled=True)  46.6 us
    all_to_all x5, starting transfers between devices, sent_and_summed(): lax.all_to_all(blocks, axis, split_axis=0, concat_axis=0, tiled=True)  33.6 us
    dot_general x16, matrix products, product(): jnp.dot(left, right, precision=precise, preferred_element_type=jnp.float32)  32.3 us
    all_to_all x4, starting transfers between devices, copy_for_each(): return lax.all_to_all(copies, axis, split_axis=0, concat_axis=0, tiled=True)  24.4 us
    all_to_all x4, waiting for transfers between devices, copy_for_each(): return lax.all_to_all(copies, axis, split_axis=0, concat_axis=0, tiled=True)  15.4 us
    all_to_all x1, blocking collectives, copy_for_each(): return lax.all_to_all(copies, axis, split_axis=0, concat_axis=0, tiled=True)  14.2 us
  transfers between devices with their start and end apart: 15, of which 12 were waited for; matrix products, arithmetic and copies ran while one was open for 10% of the time, Pallas kernels for 0%

commit v1 on v0

v1 whole, which is shorter than its diff:
```python
import functools

import jax
import jax.numpy as jnp
from jax import lax
from jax.experimental import pallas as pl
from jax.experimental.pallas import tpu as pltpu
from jax.sharding import PartitionSpec as P

NX = 4
NY = 8
TILE = 256
SUPER = 3
f32 = jnp.float32
bf16 = jnp.bfloat16


def halves(value):
    high = value.astype(bf16)
    low = (value - high.astype(f32)).astype(bf16)
    return high, low


def dot(left, right):
    return lax.dot_general(left, right, (((1,), (0,)), ((), ())), preferred_element_type=f32)


def dot_t(left, right):
    return lax.dot_general(left, right, (((1,), (1,)), ((), ())), preferred_element_type=f32)


def left_dot(left, right):
    high, low = halves(left)
    both = dot(jnp.concatenate([high, low], axis=0), right)
    return both[: left.shape[0]] + both[left.shape[0] :]


def kernel(
    nz, nc, tiles, s_ref, p_ref, l_ref, d_ref, x_out, y_out, g_out,
    sh, sl, pt, xp, xh, xl, xsib, xs, xr, cf, ct, ap, ar, ax, ay, bb, ex, tb, tt, gx, ga, yx, yf,
    psa_s, psc_s, psx_s, psa_r, psx_r, c_s, c_r, cd_s, cd_r, d2_s, d2_r, z_s, z_r,
    ar_s, ar_r, ay_s, ay_r, ex_s, ex_r, t_s, t_r, ga_s, ga_r, yx_s, yx_r,
):
    rows, depth = s_ref.shape
    wide = p_ref.shape[2]
    wc = wide // nc
    lanes = wide // NX
    cx = nc // NX
    kb = depth // 2
    r = lax.axis_index("row")
    c = lax.axis_index("col")
    x, y = lax.div(r, NY), lax.rem(r, NY)
    z, core = lax.div(c, 2), lax.rem(c, 2)
    other = 1 - core
    xt, slot = lax.div(c, cx), lax.rem(c, cx)
    my_lanes = pl.ds(pl.multiple_of(x * lanes, lanes), lanes)

    def ring(at, step, size):
        return lax.rem(at + step, size)

    pending = []

    def send(src, dst, ssem, rsem, row, col, cond=None):
        copy = pltpu.make_async_remote_copy(
            src_ref=src, dst_ref=dst, send_sem=ssem, recv_sem=rsem,
            device_id={"row": row, "col": col}, device_id_type=pl.DeviceIdType.MESH,
        )
        if cond is None:
            copy.start()
        else:
            pl.when(cond)(copy.start)
        pending.append((cond, copy))

    def arrived(dst, rsem, cond=None):
        copy = pltpu.make_async_remote_copy(
            src_ref=dst, dst_ref=dst, send_sem=rsem, recv_sem=rsem,
            device_id={"row": r, "col": c}, device_id_type=pl.DeviceIdType.MESH,
        )
        if cond is None:
            copy.wait_recv()
        else:
            pl.when(cond)(copy.wait_recv)

    def x_row(step):
        return ring(x, step, NX) * NY + y

    def y_row(step):
        return x * NY + ring(y, step, NY)

    barrier = pltpu.get_barrier_semaphore()

    def greet(row, col):
        pl.semaphore_signal(barrier, inc=1, device_id={"row": row, "col": col}, device_id_type=pl.DeviceIdType.MESH)

    for i in range(1, NX):
        greet(x_row(i), c)
    for i in range(1, NY):
        greet(y_row(i), c)
    for i in range(1, nc):
        greet(r, ring(c, i, nc))

    @pl.when(xt != x)
    def _():
        for i in range(cx):
            greet(xt * NY + y, x * cx + i)

    lane = lax.broadcasted_iota(jnp.int32, (1, rows), 1)
    mask = jnp.zeros((1, rows), f32)
    for j in range(rows // TILE):
        tile = r * (rows // TILE) + j
        hit = jnp.float32(0)
        for i in range(tiles.shape[0]):
            hit = hit + jnp.where(tiles[i] == tile, 1.0, 0.0)
        inside = jnp.where((lane >= j * TILE) & (lane < (j + 1) * TILE), 1.0, 0.0)
        mask = mask + inside * hit

    sources = [2 * c, 2 * c + 1]
    is_source = [r == src for src in sources]
    xq = [lax.div(src, NY) for src in sources]
    yq = [lax.rem(src, NY) for src in sources]
    dist = [lax.rem(y - yq[s] + NY, NY) for s in range(2)]

    for s in range(2):

        @pl.when(is_source[s])
        def _():
            for k in range(SUPER):
                turned = p_ref[k].T * mask.astype(bf16)
                pt[k, s] = turned.reshape(NX, lanes, kb)

    pl.semaphore_wait(barrier, NX - 1 + NY - 1 + nc - 1 + jnp.where(xt != x, cx, 0))

    for k in range(SUPER):
        for s in range(2):
            for i in range(1, NX):
                q = ring(x, i, NX)
                send(pt.at[k, s, q], pt.at[k, s, q], psc_s.at[k, s, i], psa_r.at[k, s], x_row(i), c, is_source[s])

    for i in range(1, nz):
        send(l_ref, cf.at[:, z, core], c_s.at[i], c_r.at[i], r, ring(z, i, nz) * 2 + core)
    cf[:, z, core] = l_ref[...]

    @pl.loop(0, rows // 128 if rows % 128 == 0 else 1)
    def _(j):
        size = 128 if rows % 128 == 0 else rows
        here = pl.ds(pl.multiple_of(j * size, size), size)
        for s in range(2):
            high, low = halves(s_ref[here, s * kb : (s + 1) * kb])
            sh[s, here] = high
            sl[s, here] = low

    def pass_on(k):
        for s in range(2):
            here = pt.at[k, s, x]
            arrived(here, psa_r.at[k, s], jnp.logical_not(is_source[s]))
            send(here, here, psa_s.at[k, s, 0], psa_r.at[k, s], y_row(1), c, dist[s] < NY // 2)
            down = (dist[s] == 0) | (dist[s] > NY // 2 + 1)
            send(here, here, psa_s.at[k, s, 1], psa_r.at[k, s], y_row(NY - 1), c, down)
            for i in range(1, NX):
                to_source = (dist[s] == 0) & (ring(x, i, NX) == xq[s])
                send(here, here, psx_s.at[k, s, i], psx_r.at[k, s, i], x_row(i), c, jnp.logical_not(to_source))

    def panel_here(k):
        for s in range(2):
            for i in range(1, NX):
                arrived(pt.at[k, s, ring(x, NX - i, NX)], psx_r.at[k, s, i], jnp.logical_not(is_source[s]))

    zx = nz // NX

    def partial(k):
        @pl.loop(0, NX)
        def _(q):
            acc = dot_t(pt[k, 0, q], sh[0]) + dot_t(pt[k, 0, q], sl[0])
            acc = acc + dot_t(pt[k, 1, q], sh[1]) + dot_t(pt[k, 1, q], sl[1])
            if k > 0:
                acc = acc + dot(ct[k - 1, q], xh[k - 1]) + dot(ct[k - 1, q], xl[k - 1])
            acc = -acc
            if k + 1 < SUPER:
                here = pl.ds(pl.multiple_of(q * lanes, lanes), lanes)
                high, low = halves(acc)
                xh[k, here] = high
                xl[k, here] = low
            xp[k, pl.ds(q * zx, zx)] = acc.reshape(zx, 2, wc, rows)

        send(xp.at[k, :, other], xsib.at[k], d2_s.at[k], d2_r.at[k], r, z * 2 + other)

    def along_z(k):
        arrived(xsib.at[k], d2_r.at[k])
        xs[k] = xp[k, :, core] + xsib[k]
        for i in range(1, nz):
            to = ring(z, i, nz)
            send(xs.at[k, to], xr.at[k, z], z_s.at[k, i], z_r.at[k, i], r, to * 2 + core)

    def summed(k):
        return wc if k + 1 == SUPER else 2 * wc

    def inverse_panel(k):
        total = xs[k, z]
        for i in range(1, nz):
            src = ring(z, nz - i, nz)
            arrived(xr.at[k, src], z_r.at[k, i])
            total = total + xr[k, src]
        total = total * mask
        x_out[k] = total
        high, low = halves(total)
        both = jnp.concatenate([high, low], axis=0)
        for j in range(k, min(k + 2, SUPER)):
            terms = dot(both, p_ref[j])
            at = (j - k) * wc
            ap[k, at : at + wc] = terms[:wc] + terms[wc:]
        n = summed(k)
        for i in range(1, NX):
            to = ring(x, i, NX)
            cut = pl.ds(pl.multiple_of(to * lanes, lanes), lanes)
            send(ap.at[k, :n, cut], ar.at[k, x, :n], ar_s.at[k, i], ar_r.at[k, i], x_row(i), c)

    def along_y(k):
        n = summed(k)
        total = ap[k, :n, my_lanes]
        for i in range(1, NX):
            src = ring(x, NX - i, NX)
            arrived(ar.at[k, src, :n], ar_r.at[k, i])
            total = total + ar[k, src, :n]
        ax[k, :n] = total
        for i in range(1, NY):
            send(ax.at[k, :n], ay.at[k, y, :n], ay_s.at[k, i], ay_r.at[k, i], y_row(i), c)

    def products(k):
        n = summed(k)
        total = ax[k, :n]
        for i in range(1, NY):
            src = ring(y, NY - i, NY)
            arrived(ay.at[k, src, :n], ay_r.at[k, i])
            total = total + ay[k, src, :n]
        bb[k, :n] = total
        ex[k, :, my_lanes] = total[:wc]
        for i in range(1, NX):
            send(bb.at[k, :wc], ex.at[k, :, my_lanes], ex_s.at[k, i], ex_r.at[k, i], x_row(i), c)
        if k + 1 < SUPER:
            for i in range(cx):
                away = (xt != x) | (slot != i)
                send(bb.at[k, wc:], tb.at[k, slot], t_s.at[k, i], t_r.at[k, slot], xt * NY + y, x * cx + i, away)

                @pl.when(jnp.logical_not(away))
                def _():
                    tb[k, i] = bb[k, wc:]

    def everyone(k):
        ga[k, c] = gx[k]
        for i in range(1, nc):
            send(gx.at[k], ga.at[k, c], ga_s.at[k, i], ga_r.at[k, i], r, ring(c, i, nc))

    def cross(k):
        for i in range(cx):
            arrived(tb.at[k, i], t_r.at[k, i], (xt != x) | (slot != i))
        tt[...] = tb[k].reshape(cx * wc, lanes).T.reshape(cx, wc, lanes)
        for i in range(1, nc):
            arrived(ga.at[k, ring(c, nc - i, nc)], ga_r.at[k, i])
        high, low = halves(ga[k].reshape(nc * wc, lanes))
        factor = ct[k, xt, pl.ds(pl.multiple_of(slot * wc, wc), wc)]
        block = -(tt[slot] + dot(factor, high) + dot(factor, low))
        yx[k] = block
        yf[k, :, my_lanes] = block
        for i in range(1, NX):
            send(yx.at[k], yf.at[k, :, my_lanes], yx_s.at[k, i], yx_r.at[k, i], x_row(i), c)

    def lanes_of(step):
        return pl.ds(pl.multiple_of(ring(x, step, NX) * lanes, lanes), lanes)

    def gathered(ref, sems, k):
        for i in range(1, NX):
            arrived(ref.at[k, :, lanes_of(NX - i)], sems.at[k, i])
        return ref[k]

    pass_on(0)
    pass_on(1)
    panel_here(0)
    partial(0)
    pass_on(2)
    along_z(0)

    for i in range(1, nz):
        arrived(cf.at[:, ring(z, nz - i, nz), core], c_r.at[i])
    send(cf.at[:, :, core], cf.at[:, :, core], cd_s.at[0], cd_r.at[0], r, z * 2 + other)
    arrived(cf.at[:, :, other], cd_r.at[0])
    for k in range(SUPER - 1):
        ct[k] = cf[k].reshape(wide, wide).T.reshape(NX, lanes, wide)

    panel_here(1)
    partial(1)
    inverse_panel(0)
    along_z(1)
    along_y(0)
    panel_here(2)
    partial(2)
    products(0)
    along_z(2)
    gx[0] = d_ref[0, :, my_lanes] - bb[0, :wc]
    everyone(0)
    inverse_panel(1)
    along_y(1)
    cross(0)
    inverse_panel(2)
    g_out[0] = d_ref[0] - gathered(ex, ex_r, 0)
    products(1)
    y_out[0] = gathered(yf, yx_r, 0)
    along_y(2)
    g_out[1] = d_ref[1] - gathered(ex, ex_r, 1) - left_dot(y_out[0], cf[0].reshape(wide, wide))
    gx[1] = g_out[1, :, my_lanes]
    everyone(1)
    products(2)
    cross(1)
    y_out[1] = gathered(yf, yx_r, 1)
    g_out[2] = d_ref[2] - gathered(ex, ex_r, 2) - left_dot(y_out[1], cf[1].reshape(wide, wide))

    for cond, copy in pending:
        if cond is None:
            copy.wait_send()
        else:
            pl.when(cond)(copy.wait_send)


def local(nz, nc, inverse_block, tile_list, panels, links, diag_inverse):
    rows, depth = inverse_block.shape
    wide = panels.shape[2]
    wc = wide // nc
    lanes = wide // NX
    cx = nc // NX
    pair = SUPER - 1
    vmem = pl.BlockSpec(memory_space=pltpu.VMEM)
    dma = pltpu.SemaphoreType.DMA
    x, y, g = pl.pallas_call(
        functools.partial(kernel, nz, nc),
        out_shape=(
            jax.ShapeDtypeStruct((SUPER, wc, rows), f32),
            jax.ShapeDtypeStruct((pair, wc, wide), f32),
            jax.ShapeDtypeStruct((SUPER, wc, wide), f32),
        ),
        in_specs=[pl.BlockSpec(memory_space=pltpu.SMEM), vmem, vmem, vmem, vmem],
        out_specs=(vmem, vmem, vmem),
        scratch_shapes=[
            pltpu.VMEM((2, rows, depth // 2), bf16),
            pltpu.VMEM((2, rows, depth // 2), bf16),
            pltpu.VMEM((SUPER, 2, NX, lanes, depth // 2), bf16),
            pltpu.VMEM((SUPER, nz, 2, wc, rows), f32),
            pltpu.VMEM((pair, wide, rows), bf16),
            pltpu.VMEM((pair, wide, rows), bf16),
            pltpu.VMEM((SUPER, nz, wc, rows), f32),
            pltpu.VMEM((SUPER, nz, wc, rows), f32),
            pltpu.VMEM((SUPER, nz, wc, rows), f32),
            pltpu.VMEM((pair, nz, 2, wc, wide), bf16),
            pltpu.VMEM((pair, NX, lanes, wide), bf16),
            pltpu.VMEM((SUPER, 2 * wc, wide), f32),
            pltpu.VMEM((SUPER, NX, 2 * wc, lanes), f32),
            pltpu.VMEM((SUPER, 2 * wc, lanes), f32),
            pltpu.VMEM((SUPER, NY, 2 * wc, lanes), f32),
            pltpu.VMEM((SUPER, 2 * wc, lanes), f32),
            pltpu.VMEM((SUPER, wc, wide), f32),
            pltpu.VMEM((pair, cx, wc, lanes), f32),
            pltpu.VMEM((cx, wc, lanes), f32),
            pltpu.VMEM((pair, wc, lanes), f32),
            pltpu.VMEM((pair, nc, wc, lanes), f32),
            pltpu.VMEM((pair, wc, lanes), f32),
            pltpu.VMEM((pair, wc, wide), f32),
            dma((SUPER, 2, 2)),
            dma((SUPER, 2, NX)),
            dma((SUPER, 2, NX)),
            dma((SUPER, 2)),
            dma((SUPER, 2, NX)),
            dma((nz,)), dma((nz,)),
            dma((1,)), dma((1,)),
            dma((SUPER,)), dma((SUPER,)),
            dma((SUPER, nz)), dma((SUPER, nz)),
            dma((SUPER, NX)), dma((SUPER, NX)),
            dma((SUPER, NY)), dma((SUPER, NY)),
            dma((SUPER, NX)), dma((SUPER, NX)),
            dma((pair, cx)), dma((pair, cx)),
            dma((pair, nc)), dma((pair, nc)),
            dma((pair, NX)), dma((pair, NX)),
        ],
        compiler_params=pltpu.CompilerParams(
            collective_id=0, has_side_effects=True, vmem_limit_bytes=60 * 1024 * 1024
        ),
    )(tile_list, inverse_block, panels, links, jnp.swapaxes(diag_inverse, 1, 2))
    return tuple(jnp.swapaxes(value, 1, 2) for value in (x, y, g))


def solution(mesh):
    nc = mesh.shape["col"]
    return jax.shard_map(
        functools.partial(local, nc // 2, nc),
        mesh=mesh,
        in_specs=(
            P("row", "col"),
            P(),
            P(None, "row", None),
            P(None, "col", None),
            P(None, None, "col"),
        ),
        out_specs=(P(None, "row", "col"), P(None, None, "col"), P(None, None, "col")),
        check_vma=False,
    )
```

time: 484 us -> 132 us (0.27)
  waiting for transfers between devices: 332 us -> 0 us
  Pallas kernels: 0 us -> 126 us
  starting transfers between devices: 58.2 us -> 0 us
  matrix products: 32.3 us -> 0 us
  other arithmetic: 17.6 us -> 0 us
  blocking collectives: 14.2 us -> 0 us
  between operations: 14.5 us -> 0.64 us
  local copies, waits for them, and re-layouts: 12.9 us -> 4.8 us
    psum x2 -> x0, waiting for transfers between devices: 181 us -> none  [from_root(): array = lax.psum(array, axis)]
    pallas_call x0 -> x1, Pallas kernels: none -> 126 us  [local(): pl.pallas_call(functools.partial(kernel, nz, nc), out_shape=(jax.ShapeDty...]
    all_to_all x9 -> x0, waiting for transfers between devices: 103 us -> none  [the longest x5 87.3 us: sent_and_summed(): lax.all_to_all(blocks, axis, split_axis=0, concat_axis=0, tiled=True)]
    all_to_all x9 -> x0, starting transfers between devices: 58 us -> none  [the longest x5 33.6 us: sent_and_summed(): lax.all_to_all(blocks, axis, split_axis=0, concat_axis=0, tiled=True)]
    all_gather x4 -> x0, waiting for transfers between devices: 46.6 us -> none  [the longest x2 46.6 us: local(): current_full = lax.all_gather(current, 'col', axis=1, tiled=True)]
    dot_general x16 -> x0, matrix products: 32.3 us -> none  [product(): jnp.dot(left, right, precision=precise, preferred_element_type=jnp.float32)]
    all_to_all x1 -> x0, blocking collectives: 14.2 us -> none  [copy_for_each(): return lax.all_to_all(copies, axis, split_axis=0, concat_axis=0, tiled=True)]
    reduce_sum x6 -> x0, other arithmetic: 6.45 us -> none  [the longest x5 4.72 us: sent_and_summed(): return arrived.sum(axis=0)]
  transfers between devices with their start and end apart: 15 -> 0, of which waited for: 12 -> 0; matrix products, arithmetic and copies ran while one was open for 10% -> 0% of each run, Pallas kernels for 0% -> 0%
where the time goes in v1:
time: 132 us; the launch traced here: 131 us
  Pallas kernels  126 us (95%)
  local copies, waits for them, and re-layouts  4.8 us (4%)
    pallas_call x1, Pallas kernels, local(): pl.pallas_call(functools.partial(kernel, nz, nc), out_shape=(jax.ShapeDty...  126 us
    unnamed x3, local copies, waits for them, and re-layouts  4.8 us

profile of v1, /device:TPU:1, one launch (start us, length us, event | category | flops | bytes accessed | tf_op | source)
XLA Modules:
  0.0 131.2 jit_solution(1357244100044850744)
XLA Ops:
  0.6 125.7 %shard_map.76 = (f32[3,32,512]{2,1,0:T(8,128)}, f32[2,32,512]{2,1,0:T(8,128)}, f32[3,32,512]{2,1,0:T(8,128)}) custom-call(s32[32]{0:T(128)} %tiles.1, f32[512,1024]{1,0:T(8,128)} %s_ref.1, bf16[3,512,512]{2,1,0:T(8,128)(2,1)} %p_ref.1, bf16[2,32,512]{2,1,0:T(8,128)(2,1)} %l_ref.1, f32[3,32,512]{2,1,0:T(8,128)} %bitcast.4), custom_call_target="tpu_custom_call" | custom-call | tf_op jit(solution)/shard_map/pallas_call | solution.py:332
  126.4 1.6 %copy.11 = f32[3,512,32]{1,2,0:T(8,128)} copy(f32[3,512,32]{1,2,0:T(8,128)} %bitcast.6) | data formatting | bytes 393216
  128.0 1.6 %copy.12 = f32[2,512,32]{1,2,0:T(8,128)} copy(f32[2,512,32]{1,2,0:T(8,128)} %bitcast.7) | data formatting | bytes 262144
  129.5 1.6 %copy.13 = f32[3,512,32]{1,2,0:T(8,128)} copy(f32[3,512,32]{1,2,0:T(8,128)} %bitcast.5) | data formatting | bytes 393216

commit v2 on v1

--- a/solution.py
+++ b/solution.py
@@ -35,11 +35,25 @@
     return both[: left.shape[0]] + both[left.shape[0] :]
 
 
+def along(size):
+    if size == 8:
+        return (((0,), 3), ((0, 1, 3), 1), ((0,), 6), ((0, 6), 7))
+    return (((0, 1), 1), ((0,), 3))
+
+
+def any_of(value, choices):
+    hit = value == choices[0]
+    for choice in choices[1:]:
+        hit = hit | (value == choice)
+    return hit
+
+
 def kernel(
-    nz, nc, tiles, s_ref, p_ref, l_ref, d_ref, x_out, y_out, g_out,
-    sh, sl, pt, xp, xh, xl, xsib, xs, xr, cf, ct, ap, ar, ax, ay, bb, ex, tb, tt, gx, ga, yx, yf,
-    psa_s, psc_s, psx_s, psa_r, psx_r, c_s, c_r, cd_s, cd_r, d2_s, d2_r, z_s, z_r,
-    ar_s, ar_r, ay_s, ay_r, ex_s, ex_r, t_s, t_r, ga_s, ga_r, yx_s, yx_r,
+    nz, nc, tiles, s_hbm, p_hbm, l_hbm, d_hbm, x_out, y_out, g_out,
+    s_ref, p_ref, l_ref, d_ref, in_s,
+    sh, sl, pt, xp, xh, xl, xsib, xs, xr, own, sc, sr, cf, ct, ap, ar, ax, ay, bb, ex, tb, tt, gx, ga, yx, yf,
+    psa_s, psc_s, psx_s, psa_r, psx_r, c_s, c_r, cd_s, cd_r, d2_s, d2_r, z_s, z_r, s_s, s_r,
+    ar_s, ar_r, ay_s, ay_r, ex_s, ex_r, t_s, t_r, ga_s, ga_r, gd_s, gd_r, yx_s, yx_r,
 ):
     rows, depth = s_ref.shape
     wide = p_ref.shape[2]
@@ -87,6 +101,13 @@
     def y_row(step):
         return x * NY + ring(y, step, NY)
 
+    loads = [
+        pltpu.make_async_copy(src, dst, in_s.at[i])
+        for i, (src, dst) in enumerate(((p_hbm, p_ref), (l_hbm, l_ref), (s_hbm, s_ref), (d_hbm, d_ref)))
+    ]
+    for load in loads:
+        load.start()
+
     barrier = pltpu.get_barrier_semaphore()
 
     def greet(row, col):
@@ -115,91 +136,131 @@
         mask = mask + inside * hit
 
     sources = [2 * c, 2 * c + 1]
-    is_source = [r == src for src in sources]
-    xq = [lax.div(src, NY) for src in sources]
-    yq = [lax.rem(src, NY) for src in sources]
-    dist = [lax.rem(y - yq[s] + NY, NY) for s in range(2)]
-
+    dist = [lax.rem(y - lax.rem(src, NY) + NY, NY) for src in sources]
+    near = jnp.where(dist[1] < dist[0], 1, 0)
+    order = []
+    for src in (near, 1 - near):
+        at = 2 * c + src
+        xs_at = lax.div(at, NY)
+        order.append((src, r == at, lax.rem(y - lax.rem(at, NY) + NY, NY), xs_at))
+
+    loads[0].wait()
     for s in range(2):
 
-        @pl.when(is_source[s])
+        @pl.when(r == sources[s])
         def _():
             for k in range(SUPER):
                 turned = p_ref[k].T * mask.astype(bf16)
-                pt[k, s] = turned.reshape(NX, lanes, kb)
+                pt[k, s] = turned.reshape(NX, 2, lanes // 2, kb)
 
     pl.semaphore_wait(barrier, NX - 1 + NY - 1 + nc - 1 + jnp.where(xt != x, cx, 0))
 
-    for k in range(SUPER):
-        for s in range(2):
-            for i in range(1, NX):
-                q = ring(x, i, NX)
-                send(pt.at[k, s, q], pt.at[k, s, q], psc_s.at[k, s, i], psa_r.at[k, s], x_row(i), c, is_source[s])
-
-    for i in range(1, nz):
-        send(l_ref, cf.at[:, z, core], c_s.at[i], c_r.at[i], r, ring(z, i, nz) * 2 + core)
-    cf[:, z, core] = l_ref[...]
-
-    @pl.loop(0, rows // 128 if rows % 128 == 0 else 1)
-    def _(j):
-        size = 128 if rows % 128 == 0 else rows
-        here = pl.ds(pl.multiple_of(j * size, size), size)
-        for s in range(2):
-            high, low = halves(s_ref[here, s * kb : (s + 1) * kb])
-            sh[s, here] = high
-            sl[s, here] = low
+    def inject(k):
+        for s, is_source, _, _ in order[:1]:
+            for h in range(2):
+                for i in (2, 1, 3) if NX == 4 else range(1, NX):
+                    q = ring(x, i, NX)
+                    here = pt.at[k, s, q, h]
+                    send(here, here, psc_s.at[k, h, i], psa_r.at[k, s, h], x_row(i), c, is_source)
 
     def pass_on(k):
-        for s in range(2):
-            here = pt.at[k, s, x]
-            arrived(here, psa_r.at[k, s], jnp.logical_not(is_source[s]))
-            send(here, here, psa_s.at[k, s, 0], psa_r.at[k, s], y_row(1), c, dist[s] < NY // 2)
-            down = (dist[s] == 0) | (dist[s] > NY // 2 + 1)
-            send(here, here, psa_s.at[k, s, 1], psa_r.at[k, s], y_row(NY - 1), c, down)
-            for i in range(1, NX):
-                to_source = (dist[s] == 0) & (ring(x, i, NX) == xq[s])
-                send(here, here, psx_s.at[k, s, i], psx_r.at[k, s, i], x_row(i), c, jnp.logical_not(to_source))
+        for j, (s, is_source, away, xq) in enumerate(order):
+            for h in range(2):
+                here = pt.at[k, s, x, h]
+                arrived(here, psa_r.at[k, s, h], jnp.logical_not(is_source))
+                for n, (senders, step) in enumerate(along(NY)):
+                    send(here, here, psa_s.at[k, j, h, n], psa_r.at[k, s, h], y_row(step), c, any_of(away, senders))
+                for i in (1, NX - 1) if NX > 2 else (1,):
+                    to_source = (away == 0) & (ring(x, i, NX) == xq)
+                    send(
+                        here, here, psx_s.at[k, j, h, i], psx_r.at[k, s, h, i], x_row(i), c, jnp.logical_not(to_source)
+                    )
+
+    def forward(k):
+        for j, (s, is_source, away, xq) in enumerate(order):
+            needed = jnp.logical_not(is_source)
+            for h in range(2):
+                for i in (1, NX - 1) if NX > 2 else (1,):
+                    there = pt.at[k, s, ring(x, NX - i, NX), h]
+                    arrived(there, psx_r.at[k, s, h, i], needed)
+                    if NX == 4 and i == (1 if h == 0 else 3):
+                        to_source = (away == 0) & (ring(x, i, NX) == xq)
+                        send(
+                            there, there, psx_s.at[k, j, h, 2], psx_r.at[k, s, h, 2], x_row(i), c,
+                            jnp.logical_not(to_source),
+                        )
 
     def panel_here(k):
-        for s in range(2):
-            for i in range(1, NX):
-                arrived(pt.at[k, s, ring(x, NX - i, NX)], psx_r.at[k, s, i], jnp.logical_not(is_source[s]))
+        if NX == 4:
+            for s, is_source, _, _ in order:
+                for h in range(2):
+                    arrived(pt.at[k, s, ring(x, 2, NX), h], psx_r.at[k, s, h, 2], jnp.logical_not(is_source))
+
+    def two_terms():
+        loads[2].wait()
+        size = min(rows, 128)
+
+        @pl.loop(0, rows // size)
+        def _(j):
+            here = pl.ds(pl.multiple_of(j * size, size), size)
+            for s in range(2):
+                high, low = halves(s_ref[here, s * kb : (s + 1) * kb])
+                sh[s, here] = high
+                sl[s, here] = low
+
+    def share_links():
+        loads[1].wait()
+        for i in range(1, nz):
+            send(l_ref, cf.at[:, z, core], c_s.at[i], c_r.at[i], r, ring(z, i, nz) * 2 + core)
+        cf[:, z, core] = l_ref[...]
 
     zx = nz // NX
 
     def partial(k):
-        @pl.loop(0, NX)
+        two = 2 * lanes
+
+        @pl.loop(0, NX // 2)
         def _(q):
-            acc = dot_t(pt[k, 0, q], sh[0]) + dot_t(pt[k, 0, q], sl[0])
-            acc = acc + dot_t(pt[k, 1, q], sh[1]) + dot_t(pt[k, 1, q], sl[1])
+            first = pt[k, 0, pl.ds(2 * q, 2)].reshape(two, kb)
+            second = pt[k, 1, pl.ds(2 * q, 2)].reshape(two, kb)
+            acc = dot_t(first, sh[0]) + dot_t(first, sl[0])
+            acc = acc + dot_t(second, sh[1]) + dot_t(second, sl[1])
             if k > 0:
-                acc = acc + dot(ct[k - 1, q], xh[k - 1]) + dot(ct[k - 1, q], xl[k - 1])
+                factor = ct[k - 1, pl.ds(2 * q, 2)].reshape(two, wide)
+                acc = acc + dot(factor, xh[k - 1]) + dot(factor, xl[k - 1])
             acc = -acc
             if k + 1 < SUPER:
-                here = pl.ds(pl.multiple_of(q * lanes, lanes), lanes)
+                here = pl.ds(pl.multiple_of(q * two, two), two)
                 high, low = halves(acc)
                 xh[k, here] = high
                 xl[k, here] = low
-            xp[k, pl.ds(q * zx, zx)] = acc.reshape(zx, 2, wc, rows)
+            xp[k, pl.ds(q * 2 * zx, 2 * zx)] = acc.reshape(2 * zx, 2, wc, rows)
 
         send(xp.at[k, :, other], xsib.at[k], d2_s.at[k], d2_r.at[k], r, z * 2 + other)
 
     def along_z(k):
         arrived(xsib.at[k], d2_r.at[k])
-        xs[k] = xp[k, :, core] + xsib[k]
+        mine = xp[k, :, core] + xsib[k]
+        own[k] = xp[k, z, core] + xsib[k, z]
+        top = jnp.max(jnp.abs(mine), axis=1, keepdims=True)
+        sc[k] = top * (1 / 32767)
+        steps = jnp.where(top > 0, 32767 / jnp.where(top > 0, top, 1.0), 0.0)
+        xs[k] = jnp.round(mine * steps).astype(jnp.int32).astype(jnp.int16)
         for i in range(1, nz):
             to = ring(z, i, nz)
+            send(sc.at[k, to], sr.at[k, z], s_s.at[k, i], s_r.at[k, i], r, to * 2 + core)
             send(xs.at[k, to], xr.at[k, z], z_s.at[k, i], z_r.at[k, i], r, to * 2 + core)
 
     def summed(k):
         return wc if k + 1 == SUPER else 2 * wc
 
     def inverse_panel(k):
-        total = xs[k, z]
+        total = own[k]
         for i in range(1, nz):
             src = ring(z, nz - i, nz)
+            arrived(sr.at[k, src], s_r.at[k, i])
             arrived(xr.at[k, src], z_r.at[k, i])
-            total = total + xr[k, src]
+            total = total + xr[k, src].astype(jnp.int32).astype(f32) * sr[k, src]
         total = total * mask
         x_out[k] = total
         high, low = halves(total)
@@ -246,16 +307,18 @@
                     tb[k, i] = bb[k, wc:]
 
     def everyone(k):
-        ga[k, c] = gx[k]
-        for i in range(1, nc):
-            send(gx.at[k], ga.at[k, c], ga_s.at[k, i], ga_r.at[k, i], r, ring(c, i, nc))
+        for i in range(1, nz):
+            send(gx.at[k], ga.at[k, z, core], ga_s.at[k, i], ga_r.at[k, i], r, ring(z, i, nz) * 2 + core)
+        ga[k, z, core] = gx[k]
 
     def cross(k):
+        for i in range(1, nz):
+            arrived(ga.at[k, ring(z, nz - i, nz), core], ga_r.at[k, i])
+        send(ga.at[k, :, core], ga.at[k, :, core], gd_s.at[k], gd_r.at[k], r, z * 2 + other)
         for i in range(cx):
             arrived(tb.at[k, i], t_r.at[k, i], (xt != x) | (slot != i))
         tt[...] = tb[k].reshape(cx * wc, lanes).T.reshape(cx, wc, lanes)
-        for i in range(1, nc):
-            arrived(ga.at[k, ring(c, nc - i, nc)], ga_r.at[k, i])
+        arrived(ga.at[k, :, other], gd_r.at[k])
         high, low = halves(ga[k].reshape(nc * wc, lanes))
         factor = ct[k, xt, pl.ds(pl.multiple_of(slot * wc, wc), wc)]
         block = -(tt[slot] + dot(factor, high) + dot(factor, low))
@@ -272,10 +335,17 @@
             arrived(ref.at[k, :, lanes_of(NX - i)], sems.at[k, i])
         return ref[k]
 
+    inject(0)
+    share_links()
     pass_on(0)
+    inject(1)
+    two_terms()
+    forward(0)
     pass_on(1)
+    inject(2)
     panel_here(0)
     partial(0)
+    forward(1)
     pass_on(2)
     along_z(0)
 
@@ -288,23 +358,25 @@
 
     panel_here(1)
     partial(1)
+    forward(2)
+    along_z(1)
     inverse_panel(0)
-    along_z(1)
-    along_y(0)
     panel_here(2)
     partial(2)
+    along_y(0)
+    along_z(2)
+    loads[3].wait()
+    inverse_panel(1)
     products(0)
-    along_z(2)
     gx[0] = d_ref[0, :, my_lanes] - bb[0, :wc]
     everyone(0)
-    inverse_panel(1)
     along_y(1)
+    inverse_panel(2)
     cross(0)
-    inverse_panel(2)
     g_out[0] = d_ref[0] - gathered(ex, ex_r, 0)
     products(1)
+    along_y(2)
     y_out[0] = gathered(yf, yx_r, 0)
-    along_y(2)
     g_out[1] = d_ref[1] - gathered(ex, ex_r, 1) - left_dot(y_out[0], cf[0].reshape(wide, wide))
     gx[1] = g_out[1, :, my_lanes]
     everyone(1)
@@ -318,6 +390,12 @@
             copy.wait_send()
         else:
             pl.when(cond)(copy.wait_send)
+
+
+def finish(x_ref, y_ref, g_ref, x_out, y_out, g_out):
+    x_out[...] = x_ref[...]
+    y_out[...] = y_ref[...]
+    g_out[...] = g_ref[...]
 
 
 def local(nz, nc, inverse_block, tile_list, panels, links, diag_inverse):
@@ -336,18 +414,26 @@
             jax.ShapeDtypeStruct((pair, wc, wide), f32),
             jax.ShapeDtypeStruct((SUPER, wc, wide), f32),
         ),
-        in_specs=[pl.BlockSpec(memory_space=pltpu.SMEM), vmem, vmem, vmem, vmem],
+        in_specs=[pl.BlockSpec(memory_space=pltpu.SMEM)] + [pl.BlockSpec(memory_space=pl.ANY)] * 4,
         out_specs=(vmem, vmem, vmem),
         scratch_shapes=[
+            pltpu.VMEM((rows, depth), f32),
+            pltpu.VMEM(panels.shape, bf16),
+            pltpu.VMEM(links.shape, bf16),
+            pltpu.VMEM((SUPER, wc, wide), f32),
+            dma((4,)),
             pltpu.VMEM((2, rows, depth // 2), bf16),
             pltpu.VMEM((2, rows, depth // 2), bf16),
-            pltpu.VMEM((SUPER, 2, NX, lanes, depth // 2), bf16),
+            pltpu.VMEM((SUPER, 2, NX, 2, lanes // 2, depth // 2), bf16),
             pltpu.VMEM((SUPER, nz, 2, wc, rows), f32),
             pltpu.VMEM((pair, wide, rows), bf16),
             pltpu.VMEM((pair, wide, rows), bf16),
             pltpu.VMEM((SUPER, nz, wc, rows), f32),
-            pltpu.VMEM((SUPER, nz, wc, rows), f32),
-            pltpu.VMEM((SUPER, nz, wc, rows), f32),
+            pltpu.VMEM((SUPER, nz, wc, rows), jnp.int16),
+            pltpu.VMEM((SUPER, nz, wc, rows), jnp.int16),
+            pltpu.VMEM((SUPER, wc, rows), f32),
+            pltpu.VMEM((SUPER, nz, 1, rows), f32),
+            pltpu.VMEM((SUPER, nz, 1, rows), f32),
             pltpu.VMEM((pair, nz, 2, wc, wide), bf16),
             pltpu.VMEM((pair, NX, lanes, wide), bf16),
             pltpu.VMEM((SUPER, 2 * wc, wide), f32),
@@ -359,29 +445,37 @@
             pltpu.VMEM((pair, cx, wc, lanes), f32),
             pltpu.VMEM((cx, wc, lanes), f32),
             pltpu.VMEM((pair, wc, lanes), f32),
-            pltpu.VMEM((pair, nc, wc, lanes), f32),
+            pltpu.VMEM((pair, nz, 2, wc, lanes), f32),
             pltpu.VMEM((pair, wc, lanes), f32),
             pltpu.VMEM((pair, wc, wide), f32),
+            dma((SUPER, 2, 2, len(along(NY)))),
+            dma((SUPER, 2, NX)),
+            dma((SUPER, 2, 2, NX)),
             dma((SUPER, 2, 2)),
-            dma((SUPER, 2, NX)),
-            dma((SUPER, 2, NX)),
-            dma((SUPER, 2)),
-            dma((SUPER, 2, NX)),
+            dma((SUPER, 2, 2, NX)),
             dma((nz,)), dma((nz,)),
             dma((1,)), dma((1,)),
             dma((SUPER,)), dma((SUPER,)),
+            dma((SUPER, nz)), dma((SUPER, nz)),
             dma((SUPER, nz)), dma((SUPER, nz)),
             dma((SUPER, NX)), dma((SUPER, NX)),
             dma((SUPER, NY)), dma((SUPER, NY)),
             dma((SUPER, NX)), dma((SUPER, NX)),
             dma((pair, cx)), dma((pair, cx)),
-            dma((pair, nc)), dma((pair, nc)),
+            dma((pair, nz)), dma((pair, nz)),
+            dma((pair,)), dma((pair,)),
             dma((pair, NX)), dma((pair, NX)),
         ],
         compiler_params=pltpu.CompilerParams(
             collective_id=0, has_side_effects=True, vmem_limit_bytes=60 * 1024 * 1024
         ),
     )(tile_list, inverse_block, panels, links, jnp.swapaxes(diag_inverse, 1, 2))
+    x, y, g = pl.pallas_call(
+        finish,
+        out_shape=tuple(jax.ShapeDtypeStruct(value.shape, f32) for value in (x, y, g)),
+        in_specs=[vmem] * 3,
+        out_specs=(vmem,) * 3,
+    )(x, y, g)
     return tuple(jnp.swapaxes(value, 1, 2) for value in (x, y, g))
 
 

time: 132 us -> 109 us (0.83)
  Pallas kernels: 126 us -> 107 us
  local copies, waits for them, and re-layouts: 4.8 us -> 0 us
    pallas_call x1, Pallas kernels: 126 us -> 105 us  [local(): pl.pallas_call(functools.partial(kernel, nz, nc), out_shape=(jax.ShapeDty...]
    unnamed x3 -> x0, local copies, waits for them, and re-layouts: 4.8 us -> none
    pallas_call x0 -> x1, Pallas kernels: none -> 1.88 us  [local(): pl.pallas_call(finish, out_shape=tuple((jax.ShapeDtypeStruct(value.shape,...]
where the time goes in v2:
time: 109 us; the launch traced here: 107 us
  Pallas kernels  107 us (98%)
    pallas_call x1, Pallas kernels, local(): pl.pallas_call(functools.partial(kernel, nz, nc), out_shape=(jax.ShapeDty...  105 us

profile of v2, /device:TPU:1, one launch (start us, length us, event | category | flops | bytes accessed | tf_op | source)
XLA Modules:
  0.0 107.4 jit_solution(1614317684238250758)
XLA Ops:
  0.6 104.9 %shard_map.76 = (f32[3,32,512]{2,1,0:T(8,128)}, f32[2,32,512]{2,1,0:T(8,128)}, f32[3,32,512]{2,1,0:T(8,128)}) custom-call(s32[32]{0:T(128)} %tiles.1, f32[512,1024]{1,0:T(8,128)} %s_hbm.1, bf16[3,512,512]{2,1,0:T(8,128)(2,1)} %p_hbm.1, bf16[2,32,512]{2,1,0:T(8,128)(2,1)} %l_hbm.1, f32[3,32,512]{2,1,0:T(8,128)} %bitcast.4), custom_call_target="tpu_custom_call" | custom-call | tf_op jit(solution)/shard_map/pallas_call | solution.py:410
  105.5 1.9 %shard_map.77 = (f32[3,32,512]{2,1,0:T(8,128)}, f32[2,32,512]{2,1,0:T(8,128)}, f32[3,32,512]{2,1,0:T(8,128)}) custom-call(f32[3,32,512]{2,1,0:T(8,128)} %get-tuple-element.9.x_ref, f32[2,32,512]{2,1,0:T(8,128)} %get-tuple-element.10.y_ref, f32[3,32,512]{2,1,0:T(8,128)} %get-tuple-element.11.g_ref), custom_call_target="tpu_custom_call" | custom-call | tf_op jit(solution)/shard_map/pallas_call | solution.py:473

commit v3 on v2

--- a/solution.py
+++ b/solution.py
@@ -37,8 +37,8 @@
 
 def along(size):
     if size == 8:
-        return (((0,), 3), ((0, 1, 3), 1), ((0,), 6), ((0, 6), 7))
-    return (((0, 1), 1), ((0,), 3))
+        return (((0,), 0, 0, 2), ((0,), 0, 0, 6), ((0, 2), 0, 3, 1), ((0, 6), 5, 0, 7))
+    return (((0, 1), 0, 0, 1), ((0,), 0, 0, 3))
 
 
 def any_of(value, choices):
@@ -49,11 +49,11 @@
 
 
 def kernel(
-    nz, nc, tiles, s_hbm, p_hbm, l_hbm, d_hbm, x_out, y_out, g_out,
-    s_ref, p_ref, l_ref, d_ref, in_s,
-    sh, sl, pt, xp, xh, xl, xsib, xs, xr, own, sc, sr, cf, ct, ap, ar, ax, ay, bb, ex, tb, tt, gx, ga, yx, yf,
-    psa_s, psc_s, psx_s, psa_r, psx_r, c_s, c_r, cd_s, cd_r, d2_s, d2_r, z_s, z_r, s_s, s_r,
-    ar_s, ar_r, ay_s, ay_r, ex_s, ex_r, t_s, t_r, ga_s, ga_r, gd_s, gd_r, yx_s, yx_r,
+    nz, nc, tiles, s_hbm, p_hbm, l_hbm, d_hbm, x_hbm, y_hbm, g_hbm,
+    s_ref, p_ref, l_ref, d_ref, x_out, y_out, g_out, in_s, out_s,
+    sh, sl, pt, xp, xh, xl, xsib, xs, xr, own, sc, sr, cf, ct, ap, ar, ax, ay, bb, ex, tb, tf, tt, gx, ga, ya, yx, yf, vc,
+    psa_s, psc_s, psx_s, psa_r, psx_r, psf_r, c_s, c_r, cd_s, cd_r, d2_s, d2_r, z_s, z_r, s_s, s_r,
+    ar_s, ar_r, ay_s, ay_r, ex_s, ex_r, t_s, t_r, tf_s, tf_r, td_s, td_r, ga_s, ga_r, gd_s, gd_r, yx_s, yx_r,
 ):
     rows, depth = s_ref.shape
     wide = p_ref.shape[2]
@@ -83,7 +83,21 @@
             copy.start()
         else:
             pl.when(cond)(copy.start)
+
+    def later(size, ssem, cond=None):
+        copy = pltpu.make_async_remote_copy(
+            src_ref=size, dst_ref=size, send_sem=ssem, recv_sem=ssem,
+            device_id={"row": r, "col": c}, device_id_type=pl.DeviceIdType.MESH,
+        )
         pending.append((cond, copy))
+
+    def drain():
+        for cond, copy in pending:
+            if cond is None:
+                copy.wait_send()
+            else:
+                pl.when(cond)(copy.wait_send)
+        pending.clear()
 
     def arrived(dst, rsem, cond=None):
         copy = pltpu.make_async_remote_copy(
@@ -108,6 +122,13 @@
     for load in loads:
         load.start()
 
+    stores = []
+
+    def put(src, dst, k):
+        store = pltpu.make_async_copy(src.at[k], dst.at[k], out_s.at[len(stores)])
+        store.start()
+        stores.append(store)
+
     barrier = pltpu.get_barrier_semaphore()
 
     def greet(row, col):
@@ -120,10 +141,10 @@
     for i in range(1, nc):
         greet(r, ring(c, i, nc))
 
-    @pl.when(xt != x)
-    def _():
-        for i in range(cx):
-            greet(xt * NY + y, x * cx + i)
+    for i in range(NX):
+        for j in range(cx):
+            here = (i == x) & (xt == x) & (j == slot)
+            pl.when(jnp.logical_not(here))(functools.partial(greet, i * NY + y, x * cx + j))
 
     lane = lax.broadcasted_iota(jnp.int32, (1, rows), 1)
     mask = jnp.zeros((1, rows), f32)
@@ -137,7 +158,9 @@
 
     sources = [2 * c, 2 * c + 1]
     dist = [lax.rem(y - lax.rem(src, NY) + NY, NY) for src in sources]
-    near = jnp.where(dist[1] < dist[0], 1, 0)
+    reach = NY // 2 - 1 + core if NY == 8 else NY // 2
+    hops = [jnp.where(d <= reach, d, NY - d) for d in dist]
+    near = jnp.where(hops[1] < hops[0], 1, 0)
     order = []
     for src in (near, 1 - near):
         at = 2 * c + src
@@ -153,7 +176,7 @@
                 turned = p_ref[k].T * mask.astype(bf16)
                 pt[k, s] = turned.reshape(NX, 2, lanes // 2, kb)
 
-    pl.semaphore_wait(barrier, NX - 1 + NY - 1 + nc - 1 + jnp.where(xt != x, cx, 0))
+    pl.semaphore_wait(barrier, NX - 1 + NY - 1 + nc - 1 + nc - jnp.where(xt == x, 1, 0))
 
     def inject(k):
         for s, is_source, _, _ in order[:1]:
@@ -161,20 +184,39 @@
                 for i in (2, 1, 3) if NX == 4 else range(1, NX):
                     q = ring(x, i, NX)
                     here = pt.at[k, s, q, h]
-                    send(here, here, psc_s.at[k, h, i], psa_r.at[k, s, h], x_row(i), c, is_source)
+                    send(here, here, psc_s.at[k], psa_r.at[k, s, h], x_row(i), c, is_source)
+            later(pt.at[k, 0, : NX - 1], psc_s.at[k], is_source)
+
+    def relay_links():
+        arrived(cf.at[:, : nz - 1, core], c_r.at[0])
+        send(cf.at[:, :, core], cf.at[:, :, core], cd_s.at[0], cd_r.at[0], r, z * 2 + other)
+        later(cf.at[:, :, core], cd_s.at[0])
+
+    def links_here():
+        arrived(cf.at[:, :, other], cd_r.at[0])
+        for k in range(SUPER - 1):
+            ct[k] = cf[k].reshape(wide, wide).T.reshape(NX, lanes, wide)
 
     def pass_on(k):
         for j, (s, is_source, away, xq) in enumerate(order):
             for h in range(2):
                 here = pt.at[k, s, x, h]
                 arrived(here, psa_r.at[k, s, h], jnp.logical_not(is_source))
-                for n, (senders, step) in enumerate(along(NY)):
-                    send(here, here, psa_s.at[k, j, h, n], psa_r.at[k, s, h], y_row(step), c, any_of(away, senders))
+                for n, (senders, more_0, more_1, step) in enumerate(along(NY)):
+                    sends = any_of(away, senders) | (away == jnp.where(core == 0, more_0, more_1))
+                    send(here, here, psa_s.at[k, j], psa_r.at[k, s, h], y_row(step), c, sends)
+                    once = sends if n == 0 else once | sends
                 for i in (1, NX - 1) if NX > 2 else (1,):
                     to_source = (away == 0) & (ring(x, i, NX) == xq)
                     send(
-                        here, here, psx_s.at[k, j, h, i], psx_r.at[k, s, h, i], x_row(i), c, jnp.logical_not(to_source)
+                        here, here, psx_s.at[k, j], psx_r.at[k, s, h, i // 2], x_row(i), c, jnp.logical_not(to_source)
                     )
+            later(pt.at[k, 0, : len(along(NY))], psa_s.at[k, j], away == 0)
+            later(pt.at[k, 0, 0], psa_s.at[k, j], once & (away != 0))
+            beside = (away == 0) & ((ring(x, 1, NX) == xq) | (ring(x, NX - 1, NX) == xq))
+            later(pt.at[k, 0, : NX - 1], psx_s.at[k, j], jnp.logical_not(beside))
+            if NX == 4:
+                later(pt.at[k, 0, :3, 0], psx_s.at[k, j], beside)
 
     def forward(k):
         for j, (s, is_source, away, xq) in enumerate(order):
@@ -182,19 +224,18 @@
             for h in range(2):
                 for i in (1, NX - 1) if NX > 2 else (1,):
                     there = pt.at[k, s, ring(x, NX - i, NX), h]
-                    arrived(there, psx_r.at[k, s, h, i], needed)
+                    arrived(there, psx_r.at[k, s, h, i // 2], needed)
                     if NX == 4 and i == (1 if h == 0 else 3):
                         to_source = (away == 0) & (ring(x, i, NX) == xq)
                         send(
-                            there, there, psx_s.at[k, j, h, 2], psx_r.at[k, s, h, 2], x_row(i), c,
+                            there, there, psx_s.at[k, j], psf_r.at[k, s], x_row(i), c,
                             jnp.logical_not(to_source),
                         )
 
     def panel_here(k):
         if NX == 4:
             for s, is_source, _, _ in order:
-                for h in range(2):
-                    arrived(pt.at[k, s, ring(x, 2, NX), h], psx_r.at[k, s, h, 2], jnp.logical_not(is_source))
+                arrived(pt.at[k, s, ring(x, 2, NX)], psf_r.at[k, s], jnp.logical_not(is_source))
 
     def two_terms():
         loads[2].wait()
@@ -211,7 +252,8 @@
     def share_links():
         loads[1].wait()
         for i in range(1, nz):
-            send(l_ref, cf.at[:, z, core], c_s.at[i], c_r.at[i], r, ring(z, i, nz) * 2 + core)
+            send(l_ref, cf.at[:, z, core], c_s.at[0], c_r.at[0], r, ring(z, i, nz) * 2 + core)
+        later(cf.at[:, : nz - 1, core], c_s.at[0])
         cf[:, z, core] = l_ref[...]
 
     zx = nz // NX
@@ -237,6 +279,7 @@
             xp[k, pl.ds(q * 2 * zx, 2 * zx)] = acc.reshape(2 * zx, 2, wc, rows)
 
         send(xp.at[k, :, other], xsib.at[k], d2_s.at[k], d2_r.at[k], r, z * 2 + other)
+        later(xsib.at[k], d2_s.at[k])
 
     def along_z(k):
         arrived(xsib.at[k], d2_r.at[k])
@@ -248,21 +291,24 @@
         xs[k] = jnp.round(mine * steps).astype(jnp.int32).astype(jnp.int16)
         for i in range(1, nz):
             to = ring(z, i, nz)
-            send(sc.at[k, to], sr.at[k, z], s_s.at[k, i], s_r.at[k, i], r, to * 2 + core)
-            send(xs.at[k, to], xr.at[k, z], z_s.at[k, i], z_r.at[k, i], r, to * 2 + core)
+            send(sc.at[k, to], sr.at[k, z], s_s.at[k], s_r.at[k], r, to * 2 + core)
+            send(xs.at[k, to], xr.at[k, z], z_s.at[k], z_r.at[k], r, to * 2 + core)
+        later(sc.at[k, : nz - 1], s_s.at[k])
+        later(xs.at[k, : nz - 1], z_s.at[k])
 
     def summed(k):
         return wc if k + 1 == SUPER else 2 * wc
 
     def inverse_panel(k):
         total = own[k]
+        arrived(sr.at[k, : nz - 1], s_r.at[k])
+        arrived(xr.at[k, : nz - 1], z_r.at[k])
         for i in range(1, nz):
             src = ring(z, nz - i, nz)
-            arrived(sr.at[k, src], s_r.at[k, i])
-            arrived(xr.at[k, src], z_r.at[k, i])
             total = total + xr[k, src].astype(jnp.int32).astype(f32) * sr[k, src]
         total = total * mask
         x_out[k] = total
+        put(x_out, x_hbm, k)
         high, low = halves(total)
         both = jnp.concatenate([high, low], axis=0)
         for j in range(k, min(k + 2, SUPER)):
@@ -273,67 +319,104 @@
         for i in range(1, NX):
             to = ring(x, i, NX)
             cut = pl.ds(pl.multiple_of(to * lanes, lanes), lanes)
-            send(ap.at[k, :n, cut], ar.at[k, x, :n], ar_s.at[k, i], ar_r.at[k, i], x_row(i), c)
+            send(ap.at[k, :n, cut], ar.at[k, x, :n], ar_s.at[k], ar_r.at[k], x_row(i), c)
+        later(ar.at[k, : NX - 1, :n], ar_s.at[k])
 
     def along_y(k):
         n = summed(k)
         total = ap[k, :n, my_lanes]
+        arrived(ar.at[k, : NX - 1, :n], ar_r.at[k])
         for i in range(1, NX):
             src = ring(x, NX - i, NX)
-            arrived(ar.at[k, src, :n], ar_r.at[k, i])
             total = total + ar[k, src, :n]
         ax[k, :n] = total
         for i in range(1, NY):
-            send(ax.at[k, :n], ay.at[k, y, :n], ay_s.at[k, i], ay_r.at[k, i], y_row(i), c)
+            send(ax.at[k, :n], ay.at[k, y, :n], ay_s.at[k], ay_r.at[k], y_row(i), c)
+        later(ay.at[k, : NY - 1, :n], ay_s.at[k])
 
     def products(k):
         n = summed(k)
         total = ax[k, :n]
+        arrived(ay.at[k, : NY - 1, :n], ay_r.at[k])
         for i in range(1, NY):
             src = ring(y, NY - i, NY)
-            arrived(ay.at[k, src, :n], ay_r.at[k, i])
             total = total + ay[k, src, :n]
         bb[k, :n] = total
         ex[k, :, my_lanes] = total[:wc]
         for i in range(1, NX):
-            send(bb.at[k, :wc], ex.at[k, :, my_lanes], ex_s.at[k, i], ex_r.at[k, i], x_row(i), c)
-        if k + 1 < SUPER:
+            send(bb.at[k, :wc], ex.at[k, :, my_lanes], ex_s.at[k], ex_r.at[k], x_row(i), c)
+        later(ex.at[k, :, : (NX - 1) * lanes], ex_s.at[k])
+        if k == 0:
+            for i in range(nz):
+                away = (xt != x) | (z != i)
+                to = tf.at[x * (cx // 2) + lax.div(slot, 2), core]
+                send(bb.at[k, wc:], to, tf_s.at[0], tf_r.at[0], xt * NY + y, i * 2 + core, away)
+            later(tf.at[:, core], tf_s.at[0], xt != x)
+            later(tf.at[: nz - 1, core], tf_s.at[0], xt == x)
+
+            @pl.when(xt == x)
+            def _():
+                tf[x * (cx // 2) + lax.div(slot, 2), core] = bb[k, wc:]
+
+        elif k + 1 < SUPER:
             for i in range(cx):
                 away = (xt != x) | (slot != i)
-                send(bb.at[k, wc:], tb.at[k, slot], t_s.at[k, i], t_r.at[k, slot], xt * NY + y, x * cx + i, away)
+                send(bb.at[k, wc:], tb.at[slot], t_s.at[0], t_r.at[0], xt * NY + y, x * cx + i, away)
 
                 @pl.when(jnp.logical_not(away))
                 def _():
-                    tb[k, i] = bb[k, wc:]
+                    tb[i] = bb[k, wc:]
+
+            later(tb, t_s.at[0], xt != x)
+            later(tb.at[: cx - 1], t_s.at[0], xt == x)
 
     def everyone(k):
+        gx[k] = d_ref[k, :, my_lanes] - bb[k, :wc]
         for i in range(1, nz):
-            send(gx.at[k], ga.at[k, z, core], ga_s.at[k, i], ga_r.at[k, i], r, ring(z, i, nz) * 2 + core)
+            send(gx.at[k], ga.at[k, z, core], ga_s.at[k], ga_r.at[k], r, ring(z, i, nz) * 2 + core)
+        later(ga.at[k, : nz - 1, core], ga_s.at[k])
         ga[k, z, core] = gx[k]
 
+    def relay(k):
+        arrived(ga.at[k, : nz - 1, core], ga_r.at[k])
+        send(ga.at[k, :, core], ga.at[k, :, core], gd_s.at[k], gd_r.at[k], r, z * 2 + other)
+        later(ga.at[k, :, core], gd_s.at[k])
+        if k == 0:
+            arrived(tf.at[:, core], tf_r.at[0], xt != x)
+            arrived(tf.at[: nz - 1, core], tf_r.at[0], xt == x)
+            send(tf.at[:, core], tf.at[:, core], td_s.at[0], td_r.at[0], r, z * 2 + other)
+            later(tf.at[:, core], td_s.at[0])
+
+    def rows_of(k):
+        return ct[k, xt, pl.ds(pl.multiple_of(slot * wc, wc), wc)]
+
     def cross(k):
-        for i in range(1, nz):
-            arrived(ga.at[k, ring(z, nz - i, nz), core], ga_r.at[k, i])
-        send(ga.at[k, :, core], ga.at[k, :, core], gd_s.at[k], gd_r.at[k], r, z * 2 + other)
-        for i in range(cx):
-            arrived(tb.at[k, i], t_r.at[k, i], (xt != x) | (slot != i))
-        tt[...] = tb[k].reshape(cx * wc, lanes).T.reshape(cx, wc, lanes)
+        n = wc
         arrived(ga.at[k, :, other], gd_r.at[k])
         high, low = halves(ga[k].reshape(nc * wc, lanes))
-        factor = ct[k, xt, pl.ds(pl.multiple_of(slot * wc, wc), wc)]
-        block = -(tt[slot] + dot(factor, high) + dot(factor, low))
-        yx[k] = block
-        yf[k, :, my_lanes] = block
+        if k == 0:
+            n = 2 * wc
+            arrived(tf.at[:, other], td_r.at[0])
+            for i in range(NX):
+                turned = tf[i * (cx // 2) : (i + 1) * (cx // 2)].reshape(lanes, lanes).T
+                total = -(turned + dot(ct[k, i], high) + dot(ct[k, i], low))
+                ya[i] = total.reshape(cx, wc, lanes)
+            yx[k, :wc] = ya[xt, slot]
+            high, low = halves(ya[...].reshape(wide, lanes))
+            yx[k, wc:] = dot(rows_of(1), high) + dot(rows_of(1), low)
+        else:
+            arrived(tb, t_r.at[0], xt != x)
+            arrived(tb.at[: cx - 1], t_r.at[0], xt == x)
+            tt[...] = tb[...].reshape(cx * wc, lanes).T.reshape(cx, wc, lanes)
+            yx[k, :wc] = vc[:, my_lanes] - (tt[slot] + dot(rows_of(k), high) + dot(rows_of(k), low))
+        yf[k, :n, my_lanes] = yx[k, :n]
         for i in range(1, NX):
-            send(yx.at[k], yf.at[k, :, my_lanes], yx_s.at[k, i], yx_r.at[k, i], x_row(i), c)
-
-    def lanes_of(step):
-        return pl.ds(pl.multiple_of(ring(x, step, NX) * lanes, lanes), lanes)
-
-    def gathered(ref, sems, k):
-        for i in range(1, NX):
-            arrived(ref.at[k, :, lanes_of(NX - i)], sems.at[k, i])
-        return ref[k]
+            send(yx.at[k, :n], yf.at[k, :n, my_lanes], yx_s.at[k], yx_r.at[k], x_row(i), c)
+        later(yf.at[k, :n, : (NX - 1) * lanes], yx_s.at[k])
+
+    def gathered(ref, sems, k, n):
+        arrived(ref.at[k, :n, : (NX - 1) * lanes], sems.at[k])
+        return ref[k, :n]
 
     inject(0)
     share_links()
@@ -345,51 +428,51 @@
     inject(2)
     panel_here(0)
     partial(0)
+    relay_links()
     forward(1)
+    along_z(0)
+    links_here()
     pass_on(2)
-    along_z(0)
-
-    for i in range(1, nz):
-        arrived(cf.at[:, ring(z, nz - i, nz), core], c_r.at[i])
-    send(cf.at[:, :, core], cf.at[:, :, core], cd_s.at[0], cd_r.at[0], r, z * 2 + other)
-    arrived(cf.at[:, :, other], cd_r.at[0])
-    for k in range(SUPER - 1):
-        ct[k] = cf[k].reshape(wide, wide).T.reshape(NX, lanes, wide)
-
     panel_here(1)
     partial(1)
-    forward(2)
     along_z(1)
     inverse_panel(0)
+    forward(2)
+    along_y(0)
     panel_here(2)
     partial(2)
-    along_y(0)
+    inverse_panel(1)
     along_z(2)
     loads[3].wait()
-    inverse_panel(1)
+    along_y(1)
     products(0)
-    gx[0] = d_ref[0, :, my_lanes] - bb[0, :wc]
     everyone(0)
-    along_y(1)
     inverse_panel(2)
+    products(1)
+    everyone(1)
+    relay(0)
     cross(0)
-    g_out[0] = d_ref[0] - gathered(ex, ex_r, 0)
-    products(1)
     along_y(2)
-    y_out[0] = gathered(yf, yx_r, 0)
-    g_out[1] = d_ref[1] - gathered(ex, ex_r, 1) - left_dot(y_out[0], cf[0].reshape(wide, wide))
-    gx[1] = g_out[1, :, my_lanes]
-    everyone(1)
+    drain()
+    g_out[0] = d_ref[0] - gathered(ex, ex_r, 0, wc)
+    put(g_out, g_hbm, 0)
+    y_out[0] = gathered(yf, yx_r, 0, 2 * wc)[:wc]
+    put(y_out, y_hbm, 0)
+    joined = left_dot(yf[0], cf[0].reshape(wide, wide))
+    vc[...] = joined[wc:]
+    g_out[1] = d_ref[1] - gathered(ex, ex_r, 1, wc) - joined[:wc]
+    put(g_out, g_hbm, 1)
+    relay(1)
+    cross(1)
     products(2)
-    cross(1)
-    y_out[1] = gathered(yf, yx_r, 1)
-    g_out[2] = d_ref[2] - gathered(ex, ex_r, 2) - left_dot(y_out[1], cf[1].reshape(wide, wide))
-
-    for cond, copy in pending:
-        if cond is None:
-            copy.wait_send()
-        else:
-            pl.when(cond)(copy.wait_send)
+    drain()
+    y_out[1] = gathered(yf, yx_r, 1, wc)
+    put(y_out, y_hbm, 1)
+    g_out[2] = d_ref[2] - gathered(ex, ex_r, 2, wc) - left_dot(y_out[1], cf[1].reshape(wide, wide))
+    put(g_out, g_hbm, 2)
+    drain()
+    for store in stores:
+        store.wait()
 
 
 def finish(x_ref, y_ref, g_ref, x_out, y_out, g_out):
@@ -415,13 +498,17 @@
             jax.ShapeDtypeStruct((SUPER, wc, wide), f32),
         ),
         in_specs=[pl.BlockSpec(memory_space=pltpu.SMEM)] + [pl.BlockSpec(memory_space=pl.ANY)] * 4,
-        out_specs=(vmem, vmem, vmem),
+        out_specs=(pl.BlockSpec(memory_space=pl.ANY),) * 3,
         scratch_shapes=[
             pltpu.VMEM((rows, depth), f32),
             pltpu.VMEM(panels.shape, bf16),
             pltpu.VMEM(links.shape, bf16),
             pltpu.VMEM((SUPER, wc, wide), f32),
+            pltpu.VMEM((SUPER, wc, rows), f32),
+            pltpu.VMEM((pair, wc, wide), f32),
+            pltpu.VMEM((SUPER, wc, wide), f32),
             dma((4,)),
+            dma((3 * SUPER - 1,)),
             pltpu.VMEM((2, rows, depth // 2), bf16),
             pltpu.VMEM((2, rows, depth // 2), bf16),
             pltpu.VMEM((SUPER, 2, NX, 2, lanes // 2, depth // 2), bf16),
@@ -442,29 +529,35 @@
             pltpu.VMEM((SUPER, NY, 2 * wc, lanes), f32),
             pltpu.VMEM((SUPER, 2 * wc, lanes), f32),
             pltpu.VMEM((SUPER, wc, wide), f32),
-            pltpu.VMEM((pair, cx, wc, lanes), f32),
+            pltpu.VMEM((cx, wc, lanes), f32),
+            pltpu.VMEM((nz, 2, wc, lanes), f32),
             pltpu.VMEM((cx, wc, lanes), f32),
             pltpu.VMEM((pair, wc, lanes), f32),
             pltpu.VMEM((pair, nz, 2, wc, lanes), f32),
-            pltpu.VMEM((pair, wc, lanes), f32),
-            pltpu.VMEM((pair, wc, wide), f32),
-            dma((SUPER, 2, 2, len(along(NY)))),
-            dma((SUPER, 2, NX)),
-            dma((SUPER, 2, 2, NX)),
+            pltpu.VMEM((NX, cx, wc, lanes), f32),
+            pltpu.VMEM((pair, 2 * wc, lanes), f32),
+            pltpu.VMEM((pair, 2 * wc, wide), f32),
+            pltpu.VMEM((wc, wide), f32),
+            dma((SUPER, 2)),
+            dma((SUPER,)),
+            dma((SUPER, 2)),
             dma((SUPER, 2, 2)),
-            dma((SUPER, 2, 2, NX)),
-            dma((nz,)), dma((nz,)),
+            dma((SUPER, 2, 2, 2)),
+            dma((SUPER, 2)),
+            dma((1,)), dma((1,)),
             dma((1,)), dma((1,)),
             dma((SUPER,)), dma((SUPER,)),
-            dma((SUPER, nz)), dma((SUPER, nz)),
-            dma((SUPER, nz)), dma((SUPER, nz)),
-            dma((SUPER, NX)), dma((SUPER, NX)),
-            dma((SUPER, NY)), dma((SUPER, NY)),
-            dma((SUPER, NX)), dma((SUPER, NX)),
-            dma((pair, cx)), dma((pair, cx)),
-            dma((pair, nz)), dma((pair, nz)),
+            dma((SUPER,)), dma((SUPER,)),
+            dma((SUPER,)), dma((SUPER,)),
+            dma((SUPER,)), dma((SUPER,)),
+            dma((SUPER,)), dma((SUPER,)),
+            dma((SUPER,)), dma((SUPER,)),
+            dma((1,)), dma((1,)),
+            dma((1,)), dma((1,)),
+            dma((1,)), dma((1,)),
             dma((pair,)), dma((pair,)),
-            dma((pair, NX)), dma((pair, NX)),
+            dma((pair,)), dma((pair,)),
+            dma((pair,)), dma((pair,)),
         ],
         compiler_params=pltpu.CompilerParams(
             collective_id=0, has_side_effects=True, vmem_limit_bytes=60 * 1024 * 1024

time: 109 us -> 100 us (0.917); the launches traced: 107 us -> 99.5 us
  Pallas kernels: 107 us -> 98.9 us
    pallas_call x1, Pallas kernels: 105 us -> 97 us  [local(): pl.pallas_call(functools.partial(kernel, nz, nc), out_shape=(jax.ShapeDty...]
where the time goes in v3:
time: 100 us; the launch traced here: 99.5 us
  Pallas kernels  98.9 us (99%)
    pallas_call x1, Pallas kernels, local(): pl.pallas_call(functools.partial(kernel, nz, nc), out_shape=(jax.ShapeDty...  97 us

profile of v3, /device:TPU:1, one launch (start us, length us, event | category | flops | bytes accessed | tf_op | source)
XLA Modules:
  0.0 99.5 jit_solution(14009275760839787277)
XLA Ops:
  0.6 97.0 %shard_map.76 = (f32[3,32,512]{2,1,0:T(8,128)}, f32[2,32,512]{2,1,0:T(8,128)}, f32[3,32,512]{2,1,0:T(8,128)}) custom-call(s32[32]{0:T(128)} %tiles.1, f32[512,1024]{1,0:T(8,128)} %s_hbm.1, bf16[3,512,512]{2,1,0:T(8,128)(2,1)} %p_hbm.1, bf16[2,32,512]{2,1,0:T(8,128)(2,1)} %l_hbm.1, f32[3,32,512]{2,1,0:T(8,128)} %bitcast.4), custom_call_target="tpu_custom_call" | custom-call | tf_op jit(solution)/shard_map/pallas_call | solution.py:493
  97.6 1.9 %shard_map.77 = (f32[3,32,512]{2,1,0:T(8,128)}, f32[2,32,512]{2,1,0:T(8,128)}, f32[3,32,512]{2,1,0:T(8,128)}) custom-call(f32[3,32,512]{2,1,0:T(8,128)} %get-tuple-element.9.x_ref, f32[2,32,512]{2,1,0:T(8,128)} %get-tuple-element.10.y_ref, f32[3,32,512]{2,1,0:T(8,128)} %get-tuple-element.11.g_ref), custom_call_target="tpu_custom_call" | custom-call | tf_op jit(solution)/shard_map/pallas_call | solution.py:566

commit v4 on v3

--- a/solution.py
+++ b/solution.py
@@ -37,8 +37,12 @@
 
 def along(size):
     if size == 8:
-        return (((0,), 0, 0, 2), ((0,), 0, 0, 6), ((0, 2), 0, 3, 1), ((0, 6), 5, 0, 7))
+        return (((0,), 0, 0, 3), ((0,), 0, 0, 6), ((0, 1, 3), 0, 0, 1), ((0, 6), 0, 0, 7))
     return (((0, 1), 0, 0, 1), ((0,), 0, 0, 3))
+
+
+def far_first(size):
+    return sorted(range(1, size), key=lambda i: -min(i, size - i))
 
 
 def any_of(value, choices):
@@ -158,7 +162,7 @@
 
     sources = [2 * c, 2 * c + 1]
     dist = [lax.rem(y - lax.rem(src, NY) + NY, NY) for src in sources]
-    reach = NY // 2 - 1 + core if NY == 8 else NY // 2
+    reach = NY // 2
     hops = [jnp.where(d <= reach, d, NY - d) for d in dist]
     near = jnp.where(hops[1] < hops[0], 1, 0)
     order = []
@@ -289,7 +293,7 @@
         sc[k] = top * (1 / 32767)
         steps = jnp.where(top > 0, 32767 / jnp.where(top > 0, top, 1.0), 0.0)
         xs[k] = jnp.round(mine * steps).astype(jnp.int32).astype(jnp.int16)
-        for i in range(1, nz):
+        for i in far_first(nz):
             to = ring(z, i, nz)
             send(sc.at[k, to], sr.at[k, z], s_s.at[k], s_r.at[k], r, to * 2 + core)
             send(xs.at[k, to], xr.at[k, z], z_s.at[k], z_r.at[k], r, to * 2 + core)
@@ -330,7 +334,7 @@
             src = ring(x, NX - i, NX)
             total = total + ar[k, src, :n]
         ax[k, :n] = total
-        for i in range(1, NY):
+        for i in far_first(NY):
             send(ax.at[k, :n], ay.at[k, y, :n], ay_s.at[k], ay_r.at[k], y_row(i), c)
         later(ay.at[k, : NY - 1, :n], ay_s.at[k])
 
@@ -372,7 +376,7 @@
 
     def everyone(k):
         gx[k] = d_ref[k, :, my_lanes] - bb[k, :wc]
-        for i in range(1, nz):
+        for i in far_first(nz):
             send(gx.at[k], ga.at[k, z, core], ga_s.at[k], ga_r.at[k], r, ring(z, i, nz) * 2 + core)
         later(ga.at[k, : nz - 1, core], ga_s.at[k])
         ga[k, z, core] = gx[k]
@@ -435,8 +439,8 @@
     pass_on(2)
     panel_here(1)
     partial(1)
+    inverse_panel(0)
     along_z(1)
-    inverse_panel(0)
     forward(2)
     along_y(0)
     panel_here(2)
@@ -444,15 +448,15 @@
     inverse_panel(1)
     along_z(2)
     loads[3].wait()
-    along_y(1)
     products(0)
     everyone(0)
+    along_y(1)
     inverse_panel(2)
     products(1)
     everyone(1)
     relay(0)
+    along_y(2)
     cross(0)
-    along_y(2)
     drain()
     g_out[0] = d_ref[0] - gathered(ex, ex_r, 0, wc)
     put(g_out, g_hbm, 0)

time: 100 us -> 98.1 us (0.981)
  Pallas kernels: 98.9 us -> 97.3 us
    pallas_call x1, Pallas kernels: 97 us -> 95.4 us  [local(): pl.pallas_call(functools.partial(kernel, nz, nc), out_shape=(jax.ShapeDty...]
where the time goes in v4:
time: 98.1 us; the launch traced here: 97.9 us
  Pallas kernels  97.3 us (99%)
    pallas_call x1, Pallas kernels, local(): pl.pallas_call(functools.partial(kernel, nz, nc), out_shape=(jax.ShapeDty...  95.4 us

profile of v4, /device:TPU:1, one launch (start us, length us, event | category | flops | bytes accessed | tf_op | source)
XLA Modules:
  0.0 97.9 jit_solution(9866053604443899097)
XLA Ops:
  0.6 95.4 %shard_map.76 = (f32[3,32,512]{2,1,0:T(8,128)}, f32[2,32,512]{2,1,0:T(8,128)}, f32[3,32,512]{2,1,0:T(8,128)}) custom-call(s32[32]{0:T(128)} %tiles.1, f32[512,1024]{1,0:T(8,128)} %s_hbm.1, bf16[3,512,512]{2,1,0:T(8,128)(2,1)} %p_hbm.1, bf16[2,32,512]{2,1,0:T(8,128)(2,1)} %l_hbm.1, f32[3,32,512]{2,1,0:T(8,128)} %bitcast.4), custom_call_target="tpu_custom_call" | custom-call | tf_op jit(solution)/shard_map/pallas_call | solution.py:497
  96.1 1.9 %shard_map.77 = (f32[3,32,512]{2,1,0:T(8,128)}, f32[2,32,512]{2,1,0:T(8,128)}, f32[3,32,512]{2,1,0:T(8,128)}) custom-call(f32[3,32,512]{2,1,0:T(8,128)} %get-tuple-element.9.x_ref, f32[2,32,512]{2,1,0:T(8,128)} %get-tuple-element.10.y_ref, f32[3,32,512]{2,1,0:T(8,128)} %get-tuple-element.11.g_ref), custom_call_target="tpu_custom_call" | custom-call | tf_op jit(solution)/shard_map/pallas_call | solution.py:570
